TPU v7x, 128 devices: a whole 4x4x4 slice. The times are simulated.
128 devices in a mesh: group: 4 (over y_hi, core), freq: 32 (over z, x, y_lo).
Axes of the slice: x: 4, y: 4 (y_hi: 2, y_lo: 2; y = y_hi * 2 + y_lo), z: 4, core: 2. Of those that a mesh axis runs over, the one named last changes fastest.
Arguments:
- spectra: bfloat16 [2048, 2, 16], P('freq', None, 'group'), may hold values from -6 to 6
- templates: bfloat16 [2048, 2, 2560], P('freq', None, 'group'), may hold values from -600 to 600
- valid_start: int32 [16], replicated, may hold values from 0 to 2048
Outputs:
- peaks: float32 [2560, 16], P('group')
All inputs are finite; a program needn't handle non-finite values.
Results may differ from a plain program's by a relative error of at most 0.0019.
Values may be sent and summed in bfloat16 or wider, within the bound.
A program may use at most 256 MiB of HBM per device.

v0:
```python
import math

import jax
import jax.numpy as jnp
from jax import lax
from jax.sharding import Mesh
from jax.sharding import PartitionSpec as P

N = 4096
VALID = 2048
FREQ = ("freq_0", "freq_1", "freq_2")


def joined_along(blocks, dim):
    shape = list(blocks.shape[1:])
    shape[dim] *= blocks.shape[0]
    return jnp.moveaxis(blocks, 0, dim).reshape(shape)


def all_blocks(x, axes, sequence):
    blocks = x[None]
    for k in sequence:
        blocks = lax.all_gather(blocks, axes[k], axis=0, tiled=True)
    carried = [lax.axis_size(axes[k]) for k in reversed(sequence)]
    blocks = blocks.reshape(*carried, *x.shape)
    turned = sorted(range(len(sequence)), key=lambda place: sequence[len(sequence) - 1 - place])
    return blocks.transpose(*turned, *range(len(sequence), blocks.ndim)).reshape(-1, *x.shape)


def gathered_by_axis(x, axes, sequence, dim):
    return joined_along(all_blocks(x, axes, sequence), dim)


def from_everyone(x, axis):
    copies = jnp.broadcast_to(x, (lax.axis_size(axis), *x.shape))
    return lax.all_to_all(copies, axis, split_axis=0, concat_axis=0, tiled=True)


def gather_directly(x, axis, dim):
    return joined_along(from_everyone(x, axis), dim)


def over_copies(x, axis):
    return from_everyone(x, axis).max(axis=0)


def make_table(bins_count, lag_index):
    bins_index = jnp.arange(bins_count, dtype=jnp.int32)
    angle = (bins_index[:, None] * lag_index[None, :] % N).astype(jnp.float32) * (2.0 * math.pi / N)
    cosine = jnp.cos(angle)
    sine_part = jnp.sin(angle)
    upper = jnp.concatenate([cosine, sine_part], 1)
    lower = jnp.concatenate([-sine_part, cosine], 1)
    return jnp.concatenate([upper, lower], 0).astype(jnp.bfloat16)


def make_cross(bank_piece, seg_piece):
    bank_re = bank_piece[:, 0, :].astype(jnp.float32)[:, None, :]
    bank_im = bank_piece[:, 1, :].astype(jnp.float32)[:, None, :]
    seg_re = seg_piece[:, 0, :].astype(jnp.float32)[:, :, None]
    seg_im = seg_piece[:, 1, :].astype(jnp.float32)[:, :, None]
    cross_re = bank_re * seg_re + bank_im * seg_im
    cross_im = bank_re * seg_im - bank_im * seg_re
    joined = jnp.stack([cross_re, cross_im], 0).astype(jnp.bfloat16)
    return joined.reshape(2 * joined.shape[1], joined.shape[2] * joined.shape[3])


def contract(cross, table):
    return lax.dot_general(
        cross, table, (((0,), (0,)), ((), ())), preferred_element_type=jnp.float32
    )


def on_device(spectra, templates, valid_start):
    freq_count = lax.axis_size(FREQ)
    lag_count = N // freq_count
    lag_index = lax.axis_index(FREQ) * lag_count + jnp.arange(lag_count, dtype=jnp.int32)
    tpl_rows = templates.shape[2]
    whole_bank = gathered_by_axis(templates, FREQ, (2, 0, 1), 0)
    whole_float = whole_bank.astype(jnp.float32)
    whole_norm = jnp.sum(whole_float * whole_float, axis=(0, 1))
    whole_table = make_table(whole_bank.shape[0], lag_index)
    every_segment = gather_directly(spectra, "group", 2)
    count = every_segment.shape[2]
    correlate_count = every_segment.shape[2]
    full_segments = gather_directly(every_segment, FREQ, 0)

    def single(strain):
        cross = make_cross(whole_bank, strain[:, :, None])
        return contract(cross, whole_table)

    series = lax.map(single, jnp.moveaxis(full_segments, 2, 0))
    series, template_norm = (series.reshape(correlate_count * tpl_rows, 2 * lag_count), whole_norm)
    power = (
        series[:, :lag_count] * series[:, :lag_count]
        + series[:, lag_count:] * series[:, lag_count:]
    )
    power = power.reshape(count, tpl_rows, lag_count) / template_norm[None, :, None]
    inside = (lag_index[None, :] >= valid_start[:, None]) & (
        lag_index[None, :] < valid_start[:, None] + VALID
    )
    peaks = jnp.max(jnp.where(inside[:, None, :], power, jnp.float32(0.0)), axis=2).T
    return over_copies(peaks, FREQ)


def solution(mesh):
    split = Mesh(
        mesh.devices.reshape(mesh.shape["group"], 4, 4, 2), ("group", "freq_0", "freq_1", "freq_2")
    )
    placed = (P(FREQ, None, "group"), P(FREQ, None, "group"), P())
    return jax.shard_map(
        on_device, mesh=split, in_specs=placed, out_specs=P("group", None), check_vma=False
    )
```

profile of v0, /device:TPU:16, one launch (start us, length us, event | category | flops | bytes accessed | tf_op | source)
XLA Modules:
  0.0 265.6 jit_solution(8880999042599202469)
XLA Ops:
  7.5 6.7 %all-gather = bf16[128,2,640]{2,0,1:T(8,128)(2,1)} all-gather(bf16[64,2,640]{2,0,1:T(8,128)(2,1)S(1)} %copy.21), channel_id=2, replica_groups=mesh['group'=4,'freq_0'=4,'freq_1'=4,'freq_2'=2] {'freq_2'}, dimensions={0}, use_global_device_ids=true | all-gather | bytes 491520 | tf_op jit(solution)/shard_map/all_gather | solution.py:23
  14.3 27.1 %all-gather.4.cloned.1.call-done = bf16[8,64,2,640]{3,1,0,2:T(8,128)(2,1)} async-done(((bf16[2,64,2,640]{3,1,0,2:T(8,128)(2,1)}), bf16[8,64,2,640]{3,1,0,2:T(8,128)(2,1)}) %all-gather.4.cloned.1.call-update) | async-done | bytes 1310736 | tf_op jit(solution)/shard_map/all_gather | solution.py:23
  42.8 4.8 %all-to-all-start = ((bf16[4,2,256]{2,1,0:T(2,128)(2,1)}), bf16[4,2,256]{2,1,0:T(2,128)(2,1)S(1)}, u32[]{:S(2)}, u32[]{:S(2)}) async-start(bf16[4,2,256]{2,1,0:T(2,128)(2,1)} %reshape.137), calls=%async_computation | async-start | bytes 8192 | tf_op jit(solution)/shard_map/all_to_all | solution.py:36
  47.6 4.4 %fusion.18 = (bf16[2048,128]{1,0:T(8,128)(2,1)S(1)}, bf16[2048,128]{1,0:T(8,128)(2,1)S(1)}, bf16[2048,128]{1,0:T(8,128)(2,1)S(1)}) fusion(s32[128]{0:T(128)S(1)} %iota_add_fusion), kind=kLoop, calls=%fused_computation.36 | loop fusion | flops 4718592 | bytes 1573376 | tf_op jit(solution)/shard_map/convert.11
  53.4 7.0 %all-to-all-start.1 = ((bf16[32,2,1024]{2,1,0:T(2,128)(2,1)}), bf16[32,2,1024]{2,1,0:T(2,128)(2,1)S(1)}, u32[]{:S(2)}, u32[]{:S(2)}) async-start(bf16[32,2,1024]{2,1,0:T(2,128)(2,1)} %reshape.139), calls=%async_computation.1 | async-start | bytes 262144 | tf_op jit(solution)/shard_map/all_to_all | solution.py:36
  60.5 10.4 %all-to-all-done.1 = bf16[32,2,1024]{2,1,0:T(2,128)(2,1)S(1)} async-done(((bf16[32,2,1024]{2,1,0:T(2,128)(2,1)}), bf16[32,2,1024]{2,1,0:T(2,128)(2,1)S(1)}, u32[]{:S(2)}, u32[]{:S(2)}) %all-to-all-start.1) | async-done | bytes 131104 | tf_op jit(solution)/shard_map/all_to_all | solution.py:36
  71.7 30.1 %all-gather.6.cloned.1.call-done = bf16[32,64,2,640]{3,1,0,2:T(8,128)(2,1)} async-done(((bf16[8,64,2,640]{3,1,0,2:T(8,128)(2,1)}), bf16[32,64,2,640]{3,1,0,2:T(8,128)(2,1)}) %all-gather.6.cloned.1.call-update) | async-done | bytes 5242896 | tf_op jit(solution)/shard_map/all_gather | solution.py:23
  101.8 5.7 %copy.23 = bf16[4,4,2,64,2,640]{5,3,2,1,0,4:T(8,128)(2,1)} copy(bf16[4,4,2,64,2,640]{5,3,2,0,1,4:T(8,128)(2,1)} %bitcast.57) | data formatting | bytes 10485760 | tf_op jit(solution)/shard_map/transpose | solution.py:27
  109.3 103.7 %while.10 = (s32[]{:T(128)}, f32[16,640,256]{2,1,0:T(8,128)}, bf16[2048,2,640]{2,0,1:T(8,128)(2,1)}, bf16[16,2048,2]{1,2,0:T(2,128)(2,1)S(1)}, bf16[4096,256]{1,0:T(8,128)(2,1)S(1)}, /*index=5*/s32[]{:T(128)}) while((s32[]{:T(128)}, f32[16,640,256]{2,1,0:T(8,128)}, bf16[2048,2,640]{2,0,1:T(8,128)(2,1)}, bf16[16,2048,2]{1,2,0:T(2,128)(2,1)S(1)}, ...), condition=%wide.region_1.2_spmd, body=%wide.region_0.0_spmd.sunk | while | flops 1357910016 | bytes 29024340 | solution.py:92
  109.4 3.5 %fusion.27 = (bf16[1,2048,1,640]{3,1,2,0:T(8,128)(2,1)S(1)}, bf16[1,2048,1,640]{3,1,2,0:T(8,128)(2,1)S(1)}) fusion(f32[2048]{0:T(1024)S(1)} %bitcast.63, f32[2048]{0:T(1024)S(1)} %bitcast.62, bf16[2048,2,640]{2,0,1:T(8,128)(2,1)} %get-tuple-element.108), kind=kLoop, calls=%fused_computation.10.clone.1 | loop fusion | flops 13107200 | bytes 10502144 | tf_op jit(solution)/shard_map/while/body/eval_jaxpr/stack | solution.py:64
  115.9 3.5 %fusion.27 = (bf16[1,2048,1,640]{3,1,2,0:T(8,128)(2,1)S(1)}, bf16[1,2048,1,640]{3,1,2,0:T(8,128)(2,1)S(1)}) fusion(f32[2048]{0:T(1024)S(1)} %bitcast.63, f32[2048]{0:T(1024)S(1)} %bitcast.62, bf16[2048,2,640]{2,0,1:T(8,128)(2,1)} %get-tuple-element.108), kind=kLoop, calls=%fused_computation.10.clone.1 | loop fusion | flops 13107200 | bytes 10502144 | tf_op jit(solution)/shard_map/while/body/eval_jaxpr/stack | solution.py:64
  122.3 3.5 %fusion.27 = (bf16[1,2048,1,640]{3,1,2,0:T(8,128)(2,1)S(1)}, bf16[1,2048,1,640]{3,1,2,0:T(8,128)(2,1)S(1)}) fusion(f32[2048]{0:T(1024)S(1)} %bitcast.63, f32[2048]{0:T(1024)S(1)} %bitcast.62, bf16[2048,2,640]{2,0,1:T(8,128)(2,1)} %get-tuple-element.108), kind=kLoop, calls=%fused_computation.10.clone.1 | loop fusion | flops 13107200 | bytes 10502144 | tf_op jit(solution)/shard_map/while/body/eval_jaxpr/stack | solution.py:64
  128.8 3.5 %fusion.27 = (bf16[1,2048,1,640]{3,1,2,0:T(8,128)(2,1)S(1)}, bf16[1,2048,1,640]{3,1,2,0:T(8,128)(2,1)S(1)}) fusion(f32[2048]{0:T(1024)S(1)} %bitcast.63, f32[2048]{0:T(1024)S(1)} %bitcast.62, bf16[2048,2,640]{2,0,1:T(8,128)(2,1)} %get-tuple-element.108), kind=kLoop, calls=%fused_computation.10.clone.1 | loop fusion | flops 13107200 | bytes 10502144 | tf_op jit(solution)/shard_map/while/body/eval_jaxpr/stack | solution.py:64
  135.3 3.5 %fusion.27 = (bf16[1,2048,1,640]{3,1,2,0:T(8,128)(2,1)S(1)}, bf16[1,2048,1,640]{3,1,2,0:T(8,128)(2,1)S(1)}) fusion(f32[2048]{0:T(1024)S(1)} %bitcast.63, f32[2048]{0:T(1024)S(1)} %bitcast.62, bf16[2048,2,640]{2,0,1:T(8,128)(2,1)} %get-tuple-element.108), kind=kLoop, calls=%fused_computation.10.clone.1 | loop fusion | flops 13107200 | bytes 10502144 | tf_op jit(solution)/shard_map/while/body/eval_jaxpr/stack | solution.py:64
  141.8 3.5 %fusion.27 = (bf16[1,2048,1,640]{3,1,2,0:T(8,128)(2,1)S(1)}, bf16[1,2048,1,640]{3,1,2,0:T(8,128)(2,1)S(1)}) fusion(f32[2048]{0:T(1024)S(1)} %bitcast.63, f32[2048]{0:T(1024)S(1)} %bitcast.62, bf16[2048,2,640]{2,0,1:T(8,128)(2,1)} %get-tuple-element.108), kind=kLoop, calls=%fused_computation.10.clone.1 | loop fusion | flops 13107200 | bytes 10502144 | tf_op jit(solution)/shard_map/while/body/eval_jaxpr/stack | solution.py:64
  148.3 3.5 %fusion.27 = (bf16[1,2048,1,640]{3,1,2,0:T(8,128)(2,1)S(1)}, bf16[1,2048,1,640]{3,1,2,0:T(8,128)(2,1)S(1)}) fusion(f32[2048]{0:T(1024)S(1)} %bitcast.63, f32[2048]{0:T(1024)S(1)} %bitcast.62, bf16[2048,2,640]{2,0,1:T(8,128)(2,1)} %get-tuple-element.108), kind=kLoop, calls=%fused_computation.10.clone.1 | loop fusion | flops 13107200 | bytes 10502144 | tf_op jit(solution)/shard_map/while/body/eval_jaxpr/stack | solution.py:64
  154.7 3.5 %fusion.27 = (bf16[1,2048,1,640]{3,1,2,0:T(8,128)(2,1)S(1)}, bf16[1,2048,1,640]{3,1,2,0:T(8,128)(2,1)S(1)}) fusion(f32[2048]{0:T(1024)S(1)} %bitcast.63, f32[2048]{0:T(1024)S(1)} %bitcast.62, bf16[2048,2,640]{2,0,1:T(8,128)(2,1)} %get-tuple-element.108), kind=kLoop, calls=%fused_computation.10.clone.1 | loop fusion | flops 13107200 | bytes 10502144 | tf_op jit(solution)/shard_map/while/body/eval_jaxpr/stack | solution.py:64
  161.2 3.5 %fusion.27 = (bf16[1,2048,1,640]{3,1,2,0:T(8,128)(2,1)S(1)}, bf16[1,2048,1,640]{3,1,2,0:T(8,128)(2,1)S(1)}) fusion(f32[2048]{0:T(1024)S(1)} %bitcast.63, f32[2048]{0:T(1024)S(1)} %bitcast.62, bf16[2048,2,640]{2,0,1:T(8,128)(2,1)} %get-tuple-element.108), kind=kLoop, calls=%fused_computation.10.clone.1 | loop fusion | flops 13107200 | bytes 10502144 | tf_op jit(solution)/shard_map/while/body/eval_jaxpr/stack | solution.py:64
  167.7 3.5 %fusion.27 = (bf16[1,2048,1,640]{3,1,2,0:T(8,128)(2,1)S(1)}, bf16[1,2048,1,640]{3,1,2,0:T(8,128)(2,1)S(1)}) fusion(f32[2048]{0:T(1024)S(1)} %bitcast.63, f32[2048]{0:T(1024)S(1)} %bitcast.62, bf16[2048,2,640]{2,0,1:T(8,128)(2,1)} %get-tuple-element.108), kind=kLoop, calls=%fused_computation.10.clone.1 | loop fusion | flops 13107200 | bytes 10502144 | tf_op jit(solution)/shard_map/while/body/eval_jaxpr/stack | solution.py:64
  174.2 3.5 %fusion.27 = (bf16[1,2048,1,640]{3,1,2,0:T(8,128)(2,1)S(1)}, bf16[1,2048,1,640]{3,1,2,0:T(8,128)(2,1)S(1)}) fusion(f32[2048]{0:T(1024)S(1)} %bitcast.63, f32[2048]{0:T(1024)S(1)} %bitcast.62, bf16[2048,2,640]{2,0,1:T(8,128)(2,1)} %get-tuple-element.108), kind=kLoop, calls=%fused_computation.10.clone.1 | loop fusion | flops 13107200 | bytes 10502144 | tf_op jit(solution)/shard_map/while/body/eval_jaxpr/stack | solution.py:64
  180.7 3.5 %fusion.27 = (bf16[1,2048,1,640]{3,1,2,0:T(8,128)(2,1)S(1)}, bf16[1,2048,1,640]{3,1,2,0:T(8,128)(2,1)S(1)}) fusion(f32[2048]{0:T(1024)S(1)} %bitcast.63, f32[2048]{0:T(1024)S(1)} %bitcast.62, bf16[2048,2,640]{2,0,1:T(8,128)(2,1)} %get-tuple-element.108), kind=kLoop, calls=%fused_computation.10.clone.1 | loop fusion | flops 13107200 | bytes 10502144 | tf_op jit(solution)/shard_map/while/body/eval_jaxpr/stack | solution.py:64
  193.6 3.5 %fusion.27 = (bf16[1,2048,1,640]{3,1,2,0:T(8,128)(2,1)S(1)}, bf16[1,2048,1,640]{3,1,2,0:T(8,128)(2,1)S(1)}) fusion(f32[2048]{0:T(1024)S(1)} %bitcast.63, f32[2048]{0:T(1024)S(1)} %bitcast.62, bf16[2048,2,640]{2,0,1:T(8,128)(2,1)} %get-tuple-element.108), kind=kLoop, calls=%fused_computation.10.clone.1 | loop fusion | flops 13107200 | bytes 10502144 | tf_op jit(solution)/shard_map/while/body/eval_jaxpr/stack | solution.py:64
  213.1 17.5 %fusion.10 = f32[10240]{0:T(1024)S(1)} fusion(f32[10240,256]{1,0:T(8,128)} %bitcast.59, f32[10240]{0:T(1024)S(1)} %div.14, pred[16,128]{1,0:T(8,128)(4,1)S(1)} %compare_and_fusion), kind=kLoop, calls=%fused_computation.22 | loop fusion | flops 7854080 | bytes 10569728 | tf_op jit(solution)/shard_map/reduce_max | solution.py:102
  230.7 27.4 %all_to_all.15 = f32[32,640,16]{1,2,0:T(8,128)S(1)} all-to-all(f32[32,640,16]{1,2,0:T(8,128)S(1)} %broadcast_in_dim.55), channel_id=1, replica_groups=mesh['group'=4,'freq_0'=4,'freq_1'=4,'freq_2'=2] {'freq_0','freq_1','fre..., dimensions={0} | all-to-all | bytes 2621440 | tf_op jit(solution)/shard_map/all_to_all | solution.py:36
  (99 shorter events, 65.1 us)
Async XLA Ops:
  6.5 45.7 %copy-start.1 = (s32[16]{0:T(128)S(1)}, s32[16]{0:T(128)}, u32[]{:S(2)}) copy-start(s32[16]{0:T(128)} %param.7) | copy-start | bytes 196
  6.5 34.9 %all-gather.4.cloned.1.call-start = ((), (), s32[]{:S(2)}) async-start(), calls=%async_computation.3 | async-start | bytes 1638400 | tf_op jit(solution)/shard_map/all_gather | solution.py:23
  14.2 87.6 %all-gather.6.cloned.1.call-start = ((), (), s32[]{:S(2)}) async-start(), calls=%async_computation.4 | async-start | bytes 6553600 | tf_op jit(solution)/shard_map/all_gather | solution.py:23
  42.8 9.5 %all-to-all-start = ((bf16[4,2,256]{2,1,0:T(2,128)(2,1)}), bf16[4,2,256]{2,1,0:T(2,128)(2,1)S(1)}, u32[]{:S(2)}, u32[]{:S(2)}) async-start(bf16[4,2,256]{2,1,0:T(2,128)(2,1)} %reshape.137), calls=%async_computation | async-start | bytes 8192 | tf_op jit(solution)/shard_map/all_to_all | solution.py:36
  53.4 17.5 %all-to-all-start.1 = ((bf16[32,2,1024]{2,1,0:T(2,128)(2,1)}), bf16[32,2,1024]{2,1,0:T(2,128)(2,1)S(1)}, u32[]{:S(2)}, u32[]{:S(2)}) async-start(bf16[32,2,1024]{2,1,0:T(2,128)(2,1)} %reshape.139), calls=%async_computation.1 | async-start | bytes 262144 | tf_op jit(solution)/shard_map/all_to_all | solution.py:36
  101.8 5.8 %copy-start = (bf16[32,64,2,640]{3,1,0,2:T(8,128)(2,1)S(1)}, bf16[32,64,2,640]{3,1,0,2:T(8,128)(2,1)}, u32[]{:S(2)}) copy-start(bf16[32,64,2,640]{3,1,0,2:T(8,128)(2,1)} %all-gather.6.cloned.1.call-done) | copy-start | bytes 15728644
Sparse Core Ops, SparseCore 0:
  14.3 26.9 all-gather.3
  43.0 58.7 all-gather.5
where the time goes:
time: 267 us; the launch traced here: 266 us
  other arithmetic  88.7 us (33%)
  waiting for transfers between devices  67.7 us (25%)
  matrix products  38.6 us (14%)
  blocking collectives  34.1 us (13%)
  between operations  13.5 us (5%)
  starting transfers between devices  11.9 us (4%)
  local copies, waits for them, and re-layouts  10.7 us (4%)
    another operation x32, other arithmetic, make_cross(): joined = jnp.stack([cross_re, cross_im], 0).astype(jnp.bfloat16)  64.4 us
    all_gather x2, waiting for transfers between devices, all_blocks(): blocks = lax.all_gather(blocks, axes[k], axis=0, tiled=True)  57.3 us
    dot_general x16, matrix products, contract(): lax.dot_general(cross, table, (((0,), (0,)), ((), ())), preferred_element...  38.6 us
    all_to_all x1, blocking collectives, from_everyone(): return lax.all_to_all(copies, axis, split_axis=0, concat_axis=0, tiled=True)  27.4 us
    reduce_max x1, other arithmetic, on_device(): jnp.max(jnp.where(inside[:, None, :], power, jnp.float32(0.0)), axis=2)  17.5 us
    all_to_all x2, starting transfers between devices, from_everyone(): return lax.all_to_all(copies, axis, split_axis=0, concat_axis=0, tiled=True)  11.8 us
    all_to_all x2, waiting for transfers between devices, from_everyone(): return lax.all_to_all(copies, axis, split_axis=0, concat_axis=0, tiled=True)  10.4 us
    all_gather x1, blocking collectives, all_blocks(): blocks = lax.all_gather(blocks, axes[k], axis=0, tiled=True)  6.71 us
  transfers between devices with their start and end apart: 4, of which 3 were waited for; matrix products, arithmetic and copies ran while one was open for 3% of the time, Pallas kernels for 0%

commit v1 on v0

v1 whole, which is shorter than its diff:
```python
import math

import jax
import jax.numpy as jnp
import numpy as np
from jax import lax
from jax.experimental import pallas as pl
from jax.experimental.pallas import tpu as pltpu
from jax.sharding import PartitionSpec as P

N = 4096
VALID = 2048
SIDE = 64
ACROSS = 32
PAIRS = 10
SEGS = 16
MESH = pl.DeviceIdType.MESH
F32 = jnp.float32
BF16 = jnp.bfloat16


def rounded_roots(index):
    exact = np.exp(2j * np.pi * (index % SIDE) / SIDE)
    least = np.full(index.shape[0], np.inf)
    table = np.zeros_like(exact)
    gain = np.ones(index.shape[0])
    for scale in np.linspace(1.0, 2.0, 2001)[:-1]:
        parts = [(x * scale).astype(jnp.bfloat16).astype(np.float64) for x in (exact.real, exact.imag)]
        tried = parts[0] + 1j * parts[1]
        level = (tried * exact.conj()).mean(1).real
        rest = (np.abs(tried / level[:, None] - exact) ** 2).mean(1)
        better = rest < least - 1e-15
        least = np.where(better, rest, least)
        table = np.where(better[:, None], tried, table)
        gain = np.where(better, level, gain)
    return table, gain


def tables():
    side = np.arange(SIDE)
    root, gain = rounded_roots(side[:, None] * np.arange(ACROSS)[None, :])
    first = np.concatenate(
        [np.concatenate([root.real, -root.imag], 1), np.concatenate([root.imag, root.real], 1)], 0
    )
    turn = np.exp(2j * np.pi * side[:, None] * side[None, :] / N) / gain[:, None]
    root, gain = rounded_roots(side[:, None] * side[None, :])
    c, s = np.kron(np.eye(2), root.real.T), np.kron(np.eye(2), root.imag.T)
    second = np.concatenate([np.concatenate([c, s], 1), np.concatenate([-s, c], 1)], 0)
    weight = np.tile(1.0 / gain ** 2, (SIDE, 2))
    turn = np.stack([np.tile(turn.real, (1, 2)), np.tile(turn.imag, (1, 2)), weight], 0)
    return jnp.asarray(first, BF16), jnp.asarray(turn, F32), jnp.asarray(second, BF16)


def kernel(
    start_ref, tpl_hbm, spec_hbm, first_hbm, turn_hbm, second_hbm, out_ref,
    tpl, spec, first, turn, second, rows, mine, got, other, beside, beside2, flat,
    bank, strain, mask, mid, peak, norm, sent, back, wide,
    load_sem, send_sem, recv_sem, recv2_sem, side_sem, side_recv, last_send, last_recv,
):
    g = lax.axis_index("group")
    f = lax.axis_index("freq")
    far = lax.rem(g + 2, 4)
    near = g + 1 - 2 * lax.rem(g, 2)
    count = 32

    loads = [
        pltpu.make_async_copy(src, dst, load_sem.at[i])
        for i, (src, dst) in enumerate(
            [(tpl_hbm, tpl), (spec_hbm, spec), (first_hbm, first), (turn_hbm, turn), (second_hbm, second)]
        )
    ]
    for load in loads:
        load.start()

    barrier = pltpu.get_barrier_semaphore()

    def greet(i, carry):
        to = lax.rem(f + i, count)
        pl.semaphore_signal(barrier, inc=1, device_id=(g, to), device_id_type=MESH)
        return carry

    def greet_far(i, carry):
        to = lax.rem(f + i, count)
        pl.semaphore_signal(barrier, inc=1, device_id=(far, to), device_id_type=MESH)
        return carry

    lax.fori_loop(1, count, greet, 0)
    lax.fori_loop(0, count, greet_far, 0)
    pl.semaphore_signal(barrier, inc=1, device_id=(near, f), device_id_type=MESH)

    for load in loads:
        load.wait()

    peak[...] = jnp.zeros_like(peak)
    norm[...] = jnp.ones_like(norm)

    for j in range(5):
        block = jnp.concatenate(
            [tpl[0, :, 128 * j:128 * (j + 1)].astype(F32), tpl[1, :, 128 * j:128 * (j + 1)].astype(F32)], 0
        )
        rows[128 * j:128 * (j + 1), :] = block.T
    own = jnp.concatenate([spec[0].astype(F32), spec[1].astype(F32)], 1).astype(BF16)

    def fill(i, carry):
        for q in range(5):
            mine[i, q] = rows[pl.ds(i + 128 * q, 4, stride=32), :].astype(BF16)
        mine[i, 5] = own
        return carry

    lax.fori_loop(0, count, fill, 0)

    lag = lax.broadcasted_iota(jnp.int32, (SIDE, 128), 0) + SIDE * (
        lax.broadcasted_iota(jnp.int32, (SIDE, 128), 1) & (SIDE - 1)
    )
    for s in range(SEGS):
        since = lag - start_ref[s]
        mask[s] = jnp.where((since >= 0) & (since < VALID), turn[2], 0.0)

    got[f] = mine[f]

    pl.semaphore_wait(barrier, 2 * count)

    def to_group(i, carry):
        to = lax.rem(f + i, count)
        pltpu.make_async_remote_copy(
            src_ref=mine.at[to], dst_ref=got.at[f], send_sem=send_sem.at[0, to], recv_sem=recv_sem.at[f],
            device_id=(g, to), device_id_type=MESH,
        ).start()
        return carry

    def to_far(i, carry):
        to = lax.rem(f + i, count)
        pltpu.make_async_remote_copy(
            src_ref=mine.at[f, 5], dst_ref=other.at[f], send_sem=send_sem.at[1, to], recv_sem=recv2_sem.at[f],
            device_id=(far, to), device_id_type=MESH,
        ).start()
        return carry

    lax.fori_loop(1, count, to_group, 0)
    lax.fori_loop(0, count, to_far, 0)

    def from_group(i, carry):
        at = lax.rem(f + i, count)
        pltpu.make_async_remote_copy(
            src_ref=mine.at[at], dst_ref=got.at[at], send_sem=send_sem.at[0, at], recv_sem=recv_sem.at[at],
            device_id=(g, at), device_id_type=MESH,
        ).wait_recv()
        return carry

    def from_far(i, carry):
        pltpu.make_async_remote_copy(
            src_ref=mine.at[f, 5], dst_ref=other.at[i], send_sem=send_sem.at[1, i], recv_sem=recv2_sem.at[i],
            device_id=(far, i), device_id_type=MESH,
        ).wait_recv()
        return carry

    lax.fori_loop(1, count, from_group, 0)
    lax.fori_loop(0, count, from_far, 0)

    side = [
        pltpu.make_async_remote_copy(
            src_ref=got.at[:, 5], dst_ref=beside, send_sem=side_sem.at[0], recv_sem=side_recv.at[0],
            device_id=(near, f), device_id_type=MESH,
        ),
        pltpu.make_async_remote_copy(
            src_ref=other, dst_ref=beside2, send_sem=side_sem.at[1], recv_sem=side_recv.at[1],
            device_id=(near, f), device_id_type=MESH,
        ),
    ]
    for copy in side:
        copy.start()

    left = lax.broadcasted_iota(jnp.int32, (ACROSS, 128), 1) < SIDE

    def swapped(x):
        return pltpu.roll(x, SIDE, 1)

    for i in range(ACROSS):
        for q in range(5):
            flat[24 * i + 4 * q:24 * i + 4 * q + 4, :] = got[i, q].astype(F32)
    for p in range(PAIRS):
        one = flat[pl.ds(p, ACROSS, stride=24), :]
        two = flat[pl.ds(p + PAIRS, ACROSS, stride=24), :]
        re = jnp.where(left, one, swapped(two))
        im = jnp.where(left, swapped(one), two)
        bank[p, 0] = re
        bank[p, 1] = im
        total = jnp.sum(re * re + im * im, axis=0, keepdims=True)
        norm[SEGS * p:SEGS * (p + 1), :] = jnp.broadcast_to(total, (SEGS, 128))

    def place(source, home):
        for i in range(ACROSS):
            flat[24 * i:24 * i + 4, :] = source(i).astype(F32)
        for q in range(4):
            row = flat[pl.ds(q, ACROSS, stride=24), :]
            turned = swapped(row)
            strain[4 * home + q, 0] = jnp.where(left, row, turned)
            strain[4 * home + q, 1] = jnp.where(left, turned, row)

    table = first[...]
    table2 = second[...]

    def correlate(groups):
        def pair(p, carry):
            h0, h1 = bank[p, 0], bank[p, 1]
            n = 0
            for home in groups:
                for half in range(2):
                    crosses = []
                    for q in range(2):
                        s = 4 * home + 2 * half + q
                        d0, d1 = strain[s, 0], strain[s, 1]
                        crosses.append(jnp.concatenate([h0 * d0 + h1 * d1, h0 * d1 - h1 * d0], 0).astype(BF16))
                    y = jnp.dot(table, jnp.concatenate(crosses, 1), preferred_element_type=F32)
                    for q in range(2):
                        re, im = y[:SIDE, 128 * q:128 * (q + 1)], y[SIDE:, 128 * q:128 * (q + 1)]
                        w0, w1 = turn[0], turn[1]
                        mid[n, :, 0:128] = (re * w0 - im * w1).astype(BF16)
                        mid[n, :, 128:256] = (re * w1 + im * w0).astype(BF16)
                        n += 1
            n = 0
            for home in groups:
                z = jnp.dot(mid[n:n + 4].reshape(4 * SIDE, 256), table2, preferred_element_type=F32)
                for q in range(4):
                    s = 4 * home + q
                    re, im = z[SIDE * q:SIDE * (q + 1), 0:128], z[SIDE * q:SIDE * (q + 1), 128:256]
                    power = (re * re + im * im) * mask[s]
                    peak[pl.ds(SEGS * p + s, 1), :] = jnp.max(power, axis=0, keepdims=True)
                    n += 1
            return carry

        lax.fori_loop(0, PAIRS, pair, 0)

    place(lambda i: got[i, 5], g)
    place(lambda i: other[i], far)
    correlate((g, far))
    for copy in side:
        copy.wait_recv()
    place(lambda i: beside[i], near)
    place(lambda i: beside2[i], lax.rem(near + 2, 4))
    correlate((near, lax.rem(near + 2, 4)))

    def halves(x, fold):
        return jnp.concatenate([fold(x[:SIDE], axis=0, keepdims=True), fold(x[SIDE:], axis=0, keepdims=True)], 0)

    for j in range(2):
        best = halves(peak[128 * j:128 * (j + 1), :].T, jnp.max)
        power = halves(norm[128 * j:128 * (j + 1), :].T, jnp.sum)
        sent[:, 128 * j:128 * (j + 1)] = best / power
    back[f] = sent[...]

    def share(i, carry):
        to = lax.rem(f + i, count)
        pltpu.make_async_remote_copy(
            src_ref=sent, dst_ref=back.at[f], send_sem=last_send.at[to], recv_sem=last_recv.at[f],
            device_id=(g, to), device_id_type=MESH,
        ).start()
        return carry

    lax.fori_loop(1, count, share, 0)

    def collect(i, carry):
        at = lax.rem(f + i, count)
        pltpu.make_async_remote_copy(
            src_ref=sent, dst_ref=back.at[at], send_sem=last_send.at[at], recv_sem=last_recv.at[at],
            device_id=(g, at), device_id_type=MESH,
        ).wait_recv()
        return carry

    lax.fori_loop(1, count, collect, 0)

    for i in range(count):
        for q in range(2):
            wide[32 * q + i:32 * q + i + 1, :] = back[i, q:q + 1, :]
    turned = [wide[:, 0:128].T, wide[:, 128:256].T]
    lane = lax.broadcasted_iota(jnp.int32, (SEGS, 128), 1)
    for c in range(5):
        block = None
        for k in range(4):
            j = 4 * c + k
            q, p = j // PAIRS, j % PAIRS
            piece = turned[p // 8][SEGS * (p % 8):SEGS * (p % 8 + 1), :]
            shift = (32 * k - 32 * q) % 128
            piece = pltpu.roll(piece, shift, 1) if shift else piece
            block = piece if block is None else jnp.where(lane >= 32 * k, piece, block)
        out_ref[:, 128 * c:128 * (c + 1)] = block

    def drain(i, carry):
        at = lax.rem(f + i, count)
        pltpu.make_async_remote_copy(
            src_ref=mine.at[at], dst_ref=got.at[f], send_sem=send_sem.at[0, at], recv_sem=recv_sem.at[f],
            device_id=(g, at), device_id_type=MESH,
        ).wait_send()
        pltpu.make_async_remote_copy(
            src_ref=sent, dst_ref=back.at[f], send_sem=last_send.at[at], recv_sem=last_recv.at[f],
            device_id=(g, at), device_id_type=MESH,
        ).wait_send()
        return carry

    def drain_far(i, carry):
        pltpu.make_async_remote_copy(
            src_ref=mine.at[f, 5], dst_ref=other.at[f], send_sem=send_sem.at[1, i], recv_sem=recv2_sem.at[f],
            device_id=(far, i), device_id_type=MESH,
        ).wait_send()
        return carry

    lax.fori_loop(1, count, drain, 0)
    lax.fori_loop(0, count, drain_far, 0)
    for copy in side:
        copy.wait_send()


def on_device(spectra, templates, valid_start):
    first, turn, second = tables()
    anywhere = pl.BlockSpec(memory_space=pl.ANY)
    dma = pltpu.SemaphoreType.DMA
    out = pl.pallas_call(
        kernel,
        out_shape=jax.ShapeDtypeStruct((SEGS, 640), F32),
        in_specs=[pl.BlockSpec(memory_space=pltpu.SMEM)] + [anywhere] * 5,
        out_specs=pl.BlockSpec(memory_space=pltpu.VMEM),
        scratch_shapes=[
            pltpu.VMEM((2, 64, 640), BF16),
            pltpu.VMEM((2, 4, 64), BF16),
            pltpu.VMEM(first.shape, BF16),
            pltpu.VMEM(turn.shape, F32),
            pltpu.VMEM(second.shape, BF16),
            pltpu.VMEM((640, 128), F32),
            pltpu.VMEM((32, 6, 4, 128), BF16),
            pltpu.VMEM((32, 6, 4, 128), BF16),
            pltpu.VMEM((32, 4, 128), BF16),
            pltpu.VMEM((32, 4, 128), BF16),
            pltpu.VMEM((32, 4, 128), BF16),
            pltpu.VMEM((32 * 24, 128), F32),
            pltpu.VMEM((PAIRS, 2, ACROSS, 128), F32),
            pltpu.VMEM((SEGS, 2, ACROSS, 128), F32),
            pltpu.VMEM((SEGS, SIDE, 128), F32),
            pltpu.VMEM((8, SIDE, 256), BF16),
            pltpu.VMEM((256, 128), F32),
            pltpu.VMEM((256, 128), F32),
            pltpu.VMEM((2, 256), F32),
            pltpu.VMEM((32, 2, 256), F32),
            pltpu.VMEM((128, 256), F32),
            dma((5,)),
            dma((2, 32)),
            dma((32,)),
            dma((32,)),
            dma((2,)),
            dma((2,)),
            dma((32,)),
            dma((32,)),
        ],
        compiler_params=pltpu.CompilerParams(collective_id=0, has_side_effects=True),
        name="matched_filter",
    )(valid_start, jnp.transpose(templates, (1, 0, 2)), jnp.transpose(spectra, (1, 2, 0)), first, turn, second)
    return out.T


def solution(mesh):
    return jax.shard_map(
        on_device, mesh=mesh, in_specs=(P("freq", None, "group"), P("freq", None, "group"), P()),
        out_specs=P("group", None), check_vma=False,
    )
```

time: 267 us -> 37.1 us (0.14)
  other arithmetic: 88.7 us -> 0 us
  waiting for transfers between devices: 67.7 us -> 0 us
  matrix products: 38.6 us -> 0 us
  blocking collectives: 34.1 us -> 0 us
  Pallas kernels: 0 us -> 33.5 us
  between operations: 13.5 us -> 0.01 us
  starting transfers between devices: 11.9 us -> 0 us
  local copies, waits for them, and re-layouts: 10.7 us -> 2.98 us
    another operation x33 -> x0, other arithmetic: 68.8 us -> none  [the longest x32 64.4 us: make_cross(): joined = jnp.stack([cross_re, cross_im], 0).astype(jnp.bfloat16)]
    all_gather x2 -> x0, waiting for transfers between devices: 57.3 us -> none  [all_blocks(): blocks = lax.all_gather(blocks, axes[k], axis=0, tiled=True)]
    dot_general x16 -> x0, matrix products: 38.6 us -> none  [contract(): lax.dot_general(cross, table, (((0,), (0,)), ((), ())), preferred_element...]
    pallas_call x0 -> x1, Pallas kernels: none -> 33.5 us  [on_device(): pl.pallas_call(kernel, out_shape=jax.ShapeDtypeStruct((SEGS, 640), F32),...]
    all_to_all x1 -> x0, blocking collectives: 27.4 us -> none  [from_everyone(): return lax.all_to_all(copies, axis, split_axis=0, concat_axis=0, tiled=True)]
    reduce_max x2 -> x0, other arithmetic: 18.2 us -> none  [the longest x1 17.5 us: on_device(): jnp.max(jnp.where(inside[:, None, :], power, jnp.float32(0.0)), axis=2)]
    all_to_all x2 -> x0, starting transfers between devices: 11.8 us -> none  [from_everyone(): return lax.all_to_all(copies, axis, split_axis=0, concat_axis=0, tiled=True)]
    all_to_all x2 -> x0, waiting for transfers between devices: 10.4 us -> none  [from_everyone(): return lax.all_to_all(copies, axis, split_axis=0, concat_axis=0, tiled=True)]
  transfers between devices with their start and end apart: 4 -> 0, of which waited for: 3 -> 0; matrix products, arithmetic and copies ran while one was open for 3% -> 0% of each run, Pallas kernels for 0% -> 0%
where the time goes in v1:
time: 37.1 us; the launch traced here: 36.5 us
  Pallas kernels  33.5 us (90%)
  local copies, waits for them, and re-layouts  2.98 us (8%)
    pallas_call x1, Pallas kernels, on_device(): pl.pallas_call(kernel, out_shape=jax.ShapeDtypeStruct((SEGS, 640), F32),...  33.5 us
    unnamed x2, local copies, waits for them, and re-layouts  2.98 us

profile of v1, /device:TPU:16, one launch (start us, length us, event | category | flops | bytes accessed | tf_op | source)
XLA Modules:
  0.0 36.5 jit_solution(13780158235922762148)
XLA Ops:
  0.0 1.6 %copy.9 = bf16[64,2,640]{2,0,1:T(8,128)(2,1)} copy(bf16[64,2,640]{2,1,0:T(2,128)(2,1)} %param.7) | data formatting | bytes 327680 | tf_op args[1]
  1.6 33.5 %matched_filter.1 = f32[16,640]{1,0:T(8,128)} custom-call(s32[16]{0:T(128)} %start_ref.1, bf16[2,64,640]{2,1,0:T(8,128)(2,1)} %bitcast.5, bf16[2,4,64]{2,1,0:T(4,128)(2,1)} %bitcast.7, bf16[128,64]{1,0:T(8,128)(2,1)} %constant.6.clone.first_hbm, f32[3,64,128]{2,1,0:T(8,128)} %constant.7.clone.turn_hbm, bf16[256,256]{1,0:T(8,128)(2,1)} %constant.8.clone.second_hbm), custom_call_target="tpu_custom_call" | custom-call | tf_op jit(solution)/shard_map/matched_filter/pallas_call | solution.py:317
  35.1 1.4 %copy.11 = f32[640,16]{0,1:T(8,128)} copy(f32[640,16]{0,1:T(8,128)} %bitcast.6) | data formatting | bytes 81920

commit v2 on v1

v2 whole, which is shorter than its diff:
```python
import math

import jax
import jax.numpy as jnp
import numpy as np
from jax import lax
from jax.experimental import pallas as pl
from jax.experimental.pallas import tpu as pltpu
from jax.sharding import PartitionSpec as P

N = 4096
VALID = 2048
SIDE = 64
ACROSS = 32
PAIRS = 10
SEGS = 16
MESH = pl.DeviceIdType.MESH
F32 = jnp.float32
BF16 = jnp.bfloat16


def rounded_roots(index):
    exact = np.exp(2j * np.pi * (index % SIDE) / SIDE)
    least = np.full(index.shape[0], np.inf)
    table = np.zeros_like(exact)
    gain = np.ones(index.shape[0])
    for scale in np.linspace(1.0, 2.0, 2001)[:-1]:
        parts = [(x * scale).astype(jnp.bfloat16).astype(np.float64) for x in (exact.real, exact.imag)]
        tried = parts[0] + 1j * parts[1]
        level = (tried * exact.conj()).mean(1).real
        rest = (np.abs(tried / level[:, None] - exact) ** 2).mean(1)
        better = rest < least - 1e-15
        least = np.where(better, rest, least)
        table = np.where(better[:, None], tried, table)
        gain = np.where(better, level, gain)
    return table, gain


def tables():
    side = np.arange(SIDE)
    root, gain = rounded_roots(side[:, None] * np.arange(ACROSS)[None, :])
    first = np.concatenate(
        [np.concatenate([root.real, -root.imag], 1), np.concatenate([root.imag, root.real], 1)], 0
    )
    turn = np.exp(2j * np.pi * side[:, None] * side[None, :] / N) / gain[:, None]
    root, gain = rounded_roots(side[:, None] * side[None, :])
    c, s = np.kron(np.eye(2), root.real.T), np.kron(np.eye(2), root.imag.T)
    second = np.concatenate([np.concatenate([c, s], 1), np.concatenate([-s, c], 1)], 0)
    weight = np.tile(1.0 / gain ** 2, (SIDE, 2))
    turn = np.stack([np.tile(turn.real, (1, 2)), np.tile(turn.imag, (1, 2)), weight], 0)
    return jnp.asarray(first, BF16), jnp.asarray(turn, F32), jnp.asarray(second, BF16)


def far_first(distance):
    offsets = [(dz, dx, dy) for dz in range(4) for dx in range(4) for dy in range(2)]
    return sorted(offsets, key=lambda o: -(min(o[0], 4 - o[0]) + min(o[1], 4 - o[1]) + distance(o[2])))


IN_GROUP = [o for o in far_first(lambda dy: dy) if o != (0, 0, 0)]
IN_FAR = far_first(lambda dy: 2 - dy)


def kernel(
    start_hbm, tpl_hbm, spec_hbm, first_hbm, turn_hbm, second_hbm, out_ref,
    start, tpl, spec, first, turn, second, rows, mine, got, other, beside, beside2, flat,
    bank, strain, mask, mid, mid2, peak, norm, sent, back, wide,
    load_sem, send_sem, recv_sem, side_sem, side_recv,
):
    g = lax.axis_index("group")
    f = lax.axis_index("freq")
    far = lax.rem(g + 2, 4)
    near = g + 1 - 2 * lax.rem(g, 2)
    count = 32
    peers = count - 1
    z, x, y = f // 8, lax.rem(f, 8) // 2, lax.rem(f, 2)
    part_z = [8 * lax.rem(z + d, 4) for d in range(4)]
    part_x = [2 * lax.rem(x + d, 4) for d in range(4)]
    part_y = [y, 1 - y]

    def at(offset):
        return part_z[offset[0]] + part_x[offset[1]] + part_y[offset[2]]

    loads = [
        pltpu.make_async_copy(src, dst, load_sem.at[i])
        for i, (src, dst) in enumerate(
            [
                (tpl_hbm, tpl), (spec_hbm, spec), (start_hbm, start),
                (first_hbm, first), (turn_hbm, turn), (second_hbm, second),
            ]
        )
    ]
    for load in loads:
        load.start()

    barrier = pltpu.get_barrier_semaphore()
    for o in IN_FAR:
        pl.semaphore_signal(barrier, inc=1, device_id=(far, at(o)), device_id_type=MESH)
    for o in IN_GROUP:
        pl.semaphore_signal(barrier, inc=1, device_id=(g, at(o)), device_id_type=MESH)
    pl.semaphore_signal(barrier, inc=1, device_id=(near, f), device_id_type=MESH)

    for load in loads:
        load.wait()

    peak[...] = jnp.zeros_like(peak)
    norm[...] = jnp.ones_like(norm)

    for j in range(5):
        block = jnp.concatenate(
            [tpl[:, q, 128 * j:128 * (j + 1)].astype(F32) for q in range(2)], 0
        )
        rows[128 * j:128 * (j + 1), :] = block.T
    own = jnp.concatenate([spec[0].astype(F32), spec[1].astype(F32)], 1).astype(BF16)

    def fill(i, carry):
        for q in range(5):
            mine[i, q] = rows[pl.ds(i + 128 * q, 4, stride=32), :].astype(BF16)
        mine[i, 5] = own
        return carry

    lax.fori_loop(0, count, fill, 0)

    lag = lax.broadcasted_iota(jnp.int32, (SIDE, 128), 0) + SIDE * (
        lax.broadcasted_iota(jnp.int32, (SIDE, 128), 1) & (SIDE - 1)
    )
    for s in range(SEGS):
        since = lag - start[s]
        mask[s] = jnp.where((since >= 0) & (since < VALID), turn[2], 0.0)

    got[f] = mine[f]

    pl.semaphore_wait(barrier, 2 * count)

    def to_far(to):
        return pltpu.make_async_remote_copy(
            src_ref=mine.at[f, 5], dst_ref=other.at[f], send_sem=send_sem.at[1], recv_sem=recv_sem.at[1],
            device_id=(far, to), device_id_type=MESH,
        )

    def to_group(to):
        return pltpu.make_async_remote_copy(
            src_ref=mine.at[to], dst_ref=got.at[f], send_sem=send_sem.at[0], recv_sem=recv_sem.at[0],
            device_id=(g, to), device_id_type=MESH,
        )

    for o in IN_FAR[:1]:
        to_far(at(o)).start()
    for o in IN_GROUP:
        to_group(at(o)).start()
    for o in IN_FAR[1:]:
        to_far(at(o)).start()

    all_group = pltpu.make_async_remote_copy(
        src_ref=mine.at[pl.ds(0, peers)], dst_ref=got.at[pl.ds(0, peers)], send_sem=send_sem.at[0],
        recv_sem=recv_sem.at[0], device_id=(near, f), device_id_type=MESH,
    )
    all_far = pltpu.make_async_remote_copy(
        src_ref=other, dst_ref=other, send_sem=send_sem.at[1],
        recv_sem=recv_sem.at[1], device_id=(near, f), device_id_type=MESH,
    )
    side = [
        pltpu.make_async_remote_copy(
            src_ref=src, dst_ref=dst, send_sem=side_sem.at[i], recv_sem=side_recv.at[i],
            device_id=(near, f), device_id_type=MESH,
        )
        for i, (src, dst) in enumerate([(got.at[:, 5], beside), (other, beside2)])
    ]
    all_group.wait_recv()
    side[0].start()

    left = lax.broadcasted_iota(jnp.int32, (ACROSS, 128), 1) < SIDE

    def swapped(x):
        return pltpu.roll(x, SIDE, 1)

    for i in range(ACROSS):
        for q in range(5):
            flat[24 * i + 4 * q:24 * i + 4 * q + 4, :] = got[i, q].astype(F32)
    for p in range(PAIRS):
        one = flat[pl.ds(p, ACROSS, stride=24), :]
        two = flat[pl.ds(p + PAIRS, ACROSS, stride=24), :]
        re = jnp.where(left, one, swapped(two))
        im = jnp.where(left, swapped(one), two)
        bank[p, 0] = re
        bank[p, 1] = im
        total = jnp.sum(re * re + im * im, axis=0, keepdims=True)
        norm[SEGS * p:SEGS * (p + 1), :] = jnp.broadcast_to(total, (SEGS, 128))

    def place(source, home):
        for i in range(ACROSS):
            flat[24 * i:24 * i + 4, :] = source(i).astype(F32)
        for q in range(4):
            row = flat[pl.ds(q, ACROSS, stride=24), :]
            turned = swapped(row)
            strain[4 * home + q, 0] = jnp.where(left, row, turned)
            strain[4 * home + q, 1] = jnp.where(left, turned, row)

    table = first[...]
    table2 = second[...]

    def across(p, homes, dst):
        h0, h1 = bank[p, 0], bank[p, 1]
        for n in range(2 * len(homes)):
            crosses = []
            for q in range(2):
                s = 4 * homes[n // 2] + 2 * (n % 2) + q
                d0, d1 = strain[s, 0], strain[s, 1]
                crosses.append(jnp.concatenate([h0 * d0 + h1 * d1, h0 * d1 - h1 * d0], 0).astype(BF16))
            y = jnp.dot(table, jnp.concatenate(crosses, 1), preferred_element_type=F32)
            for q in range(2):
                re, im = y[:SIDE, 128 * q:128 * (q + 1)], y[SIDE:, 128 * q:128 * (q + 1)]
                w0, w1 = turn[0], turn[1]
                dst[2 * n + q, :, 0:128] = (re * w0 - im * w1).astype(BF16)
                dst[2 * n + q, :, 128:256] = (re * w1 + im * w0).astype(BF16)

    def along(p, homes, src):
        for n, home in enumerate(homes):
            z = jnp.dot(src[4 * n:4 * n + 4].reshape(4 * SIDE, 256), table2, preferred_element_type=F32)
            for q in range(4):
                s = 4 * home + q
                re, im = z[SIDE * q:SIDE * (q + 1), 0:128], z[SIDE * q:SIDE * (q + 1), 128:256]
                power = (re * re + im * im) * mask[s]
                peak[pl.ds(SEGS * p + s, 1), :] = jnp.max(power, axis=0, keepdims=True)

    def steps(homes):
        def pair(i, carry):
            across(2 * i + 1, homes, mid2)
            along(2 * i, homes, mid)
            across(2 * i + 2, homes, mid)
            along(2 * i + 1, homes, mid2)
            return carry

        lax.fori_loop(0, PAIRS // 2 - 1, pair, 0)

    here, there = (g, far), (near, lax.rem(near + 2, 4))
    place(lambda i: got[i, 5], g)
    all_far.wait_recv()
    side[1].start()
    place(lambda i: other[i], far)
    across(0, here, mid)
    steps(here)
    for copy in side:
        copy.wait_recv()
    place(lambda i: beside[i], there[0])
    place(lambda i: beside2[i], there[1])
    across(PAIRS - 1, here, mid2)
    along(PAIRS - 2, here, mid)
    across(0, there, mid)
    along(PAIRS - 1, here, mid2)
    steps(there)
    across(PAIRS - 1, there, mid2)
    along(PAIRS - 2, there, mid)
    along(PAIRS - 1, there, mid2)

    def halves(x, fold):
        return jnp.concatenate([fold(x[:SIDE], axis=0, keepdims=True), fold(x[SIDE:], axis=0, keepdims=True)], 0)

    for j in range(2):
        best = halves(peak[128 * j:128 * (j + 1), :].T, jnp.max)
        power = halves(norm[128 * j:128 * (j + 1), :].T, jnp.sum)
        sent[:, 128 * j:128 * (j + 1)] = best / power
    back[f] = sent[...]

    def share(to):
        return pltpu.make_async_remote_copy(
            src_ref=sent, dst_ref=back.at[f], send_sem=send_sem.at[2], recv_sem=recv_sem.at[2],
            device_id=(g, to), device_id_type=MESH,
        )

    for o in IN_GROUP:
        share(at(o)).start()
    all_group.wait_send()
    all_far.wait_send()
    for copy in side:
        copy.wait_send()
    all_shared = pltpu.make_async_remote_copy(
        src_ref=back.at[pl.ds(0, peers)], dst_ref=back.at[pl.ds(0, peers)], send_sem=send_sem.at[2],
        recv_sem=recv_sem.at[2], device_id=(near, f), device_id_type=MESH,
    )
    all_shared.wait_recv()

    for i in range(count):
        for q in range(2):
            wide[32 * q + i:32 * q + i + 1, :] = back[i, q:q + 1, :]
    turned = [wide[:, 0:128].T, wide[:, 128:256].T]
    lane = lax.broadcasted_iota(jnp.int32, (SEGS, 128), 1)
    for c in range(5):
        block = None
        for k in range(4):
            j = 4 * c + k
            q, p = j // PAIRS, j % PAIRS
            piece = turned[p // 8][SEGS * (p % 8):SEGS * (p % 8 + 1), :]
            shift = (32 * k - 32 * q) % 128
            piece = pltpu.roll(piece, shift, 1) if shift else piece
            block = piece if block is None else jnp.where(lane >= 32 * k, piece, block)
        out_ref[:, 128 * c:128 * (c + 1)] = block

    all_shared.wait_send()


def on_device(spectra, templates, valid_start):
    first, turn, second = tables()
    anywhere = pl.BlockSpec(memory_space=pl.ANY)
    dma = pltpu.SemaphoreType.DMA
    out = pl.pallas_call(
        kernel,
        out_shape=jax.ShapeDtypeStruct((SEGS, 640), F32),
        in_specs=[anywhere] * 6,
        out_specs=pl.BlockSpec(memory_space=pltpu.VMEM),
        scratch_shapes=[
            pltpu.SMEM((SEGS,), jnp.int32),
            pltpu.VMEM((64, 2, 640), BF16),
            pltpu.VMEM((2, 4, 64), BF16),
            pltpu.VMEM(first.shape, BF16),
            pltpu.VMEM(turn.shape, F32),
            pltpu.VMEM(second.shape, BF16),
            pltpu.VMEM((640, 128), F32),
            pltpu.VMEM((32, 6, 4, 128), BF16),
            pltpu.VMEM((32, 6, 4, 128), BF16),
            pltpu.VMEM((32, 4, 128), BF16),
            pltpu.VMEM((32, 4, 128), BF16),
            pltpu.VMEM((32, 4, 128), BF16),
            pltpu.VMEM((32 * 24, 128), F32),
            pltpu.VMEM((PAIRS, 2, ACROSS, 128), F32),
            pltpu.VMEM((SEGS, 2, ACROSS, 128), F32),
            pltpu.VMEM((SEGS, SIDE, 128), F32),
            pltpu.VMEM((8, SIDE, 256), BF16),
            pltpu.VMEM((8, SIDE, 256), BF16),
            pltpu.VMEM((256, 128), F32),
            pltpu.VMEM((256, 128), F32),
            pltpu.VMEM((2, 256), F32),
            pltpu.VMEM((32, 2, 256), F32),
            pltpu.VMEM((128, 256), F32),
            dma((6,)),
            dma((3,)),
            dma((3,)),
            dma((2,)),
            dma((2,)),
        ],
        compiler_params=pltpu.CompilerParams(collective_id=0, has_side_effects=True),
        name="matched_filter",
    )(valid_start, templates, jnp.transpose(spectra, (1, 2, 0)), first, turn, second)
    return jnp.maximum(out, 0.0).T


def solution(mesh):
    return jax.shard_map(
        on_device, mesh=mesh, in_specs=(P("freq", None, "group"), P("freq", None, "group"), P()),
        out_specs=P("group", None), check_vma=False,
    )
```

time: 37.1 us -> 28.3 us (0.76)
  the two profiles are of different devices: /device:TPU:16 before, /device:TPU:0 now
where the time goes in v2:
time: 28.3 us; the launch traced here: 28.1 us
  Pallas kernels  26.7 us (94%)
  other arithmetic  1.4 us (5%)
    pallas_call x1, Pallas kernels, on_device(): pl.pallas_call(kernel, out_shape=jax.ShapeDtypeStruct((SEGS, 640), F32),...  26.7 us
    transpose x1, other arithmetic, on_device(): return jnp.maximum(out, 0.0).T  1.4 us

profile of v2, /device:TPU:0, one launch (start us, length us, event | category | flops | bytes accessed | tf_op | source)
XLA Modules:
  0.0 28.1 jit_solution(11573109094142322020)
XLA Ops:
  0.0 26.7 %matched_filter.1 = f32[16,640]{1,0:T(8,128)} custom-call(s32[16]{0:T(128)} %start_hbm.1, bf16[64,2,640]{2,1,0:T(2,128)(2,1)} %tpl_hbm.1, bf16[2,4,64]{2,1,0:T(4,128)(2,1)} %bitcast.3, bf16[128,64]{1,0:T(8,128)(2,1)} %constant.8.clone.first_hbm, f32[3,64,128]{2,1,0:T(8,128)} %constant.9.clone.turn_hbm, bf16[256,256]{1,0:T(8,128)(2,1)} %constant.10.clone.second_hbm), custom_call_target="tpu_custom_call" | custom-call | tf_op jit(solution)/shard_map/matched_filter/pallas_call | solution.py:305
  26.7 1.4 %maximum_bitcast_fusion = f32[640,16]{0,1:T(8,128)} fusion(f32[16,640]{1,0:T(8,128)} %matched_filter.1), kind=kLoop, calls=%fused_computation | loop fusion | flops 10240 | bytes 81920 | tf_op jit(solution)/shard_map/transpose | solution.py:343

commit v3 on v2

--- a/solution.py
+++ b/solution.py
@@ -39,16 +39,25 @@
 def tables():
     side = np.arange(SIDE)
     root, gain = rounded_roots(side[:, None] * np.arange(ACROSS)[None, :])
-    first = np.concatenate(
-        [np.concatenate([root.real, -root.imag], 1), np.concatenate([root.imag, root.real], 1)], 0
-    )
-    turn = np.exp(2j * np.pi * side[:, None] * side[None, :] / N) / gain[:, None]
-    root, gain = rounded_roots(side[:, None] * side[None, :])
+    first = np.stack([np.concatenate([root.real, -root.imag], 1), np.concatenate([root.imag, root.real], 1)], 0)
+    first = np.tile(first, (1, 2, 1))
+    lag = np.arange(2 * SIDE)
+    turn = np.exp(2j * np.pi * lag[:, None] * side[None, :] / N) / np.tile(gain, 2)[:, None]
+    turn = np.tile(np.stack([turn.real, turn.imag], 0), (1, 1, 2))
+    root, gain = rounded_roots(side[:VALID // SIDE, None] * side[None, :])
     c, s = np.kron(np.eye(2), root.real.T), np.kron(np.eye(2), root.imag.T)
-    second = np.concatenate([np.concatenate([c, s], 1), np.concatenate([-s, c], 1)], 0)
-    weight = np.tile(1.0 / gain ** 2, (SIDE, 2))
-    turn = np.stack([np.tile(turn.real, (1, 2)), np.tile(turn.imag, (1, 2)), weight], 0)
-    return jnp.asarray(first, BF16), jnp.asarray(turn, F32), jnp.asarray(second, BF16)
+    none = np.zeros_like(c)
+    second = np.concatenate(
+        [
+            np.concatenate([c, none, s, none], 1), np.concatenate([-s, none, c, none], 1),
+            np.concatenate([none, c, none, s], 1), np.concatenate([none, -s, none, c], 1),
+        ], 0,
+    )
+    jump = np.exp(2j * np.pi * np.arange(40)[:, None] * side[None, :] / SIDE)
+    jump = np.tile(np.stack([jump.real, jump.imag], 0), (1, 1, 2))
+    weight = np.tile(1.0 / gain ** 2, (2, 8, 4))
+    jump = np.concatenate([jump, weight], 1)
+    return jnp.asarray(first, F32), jnp.asarray(turn, F32), jnp.asarray(jump, F32), jnp.asarray(second, BF16)
 
 
 def far_first(distance):
@@ -61,9 +70,9 @@
 
 
 def kernel(
-    start_hbm, tpl_hbm, spec_hbm, first_hbm, turn_hbm, second_hbm, out_ref,
-    start, tpl, spec, first, turn, second, rows, mine, got, other, beside, beside2, flat,
-    bank, strain, mask, mid, mid2, peak, norm, sent, back, wide,
+    start_hbm, tpl_hbm, spec_hbm, first_hbm, turn_hbm, jump_hbm, second_hbm, out_ref,
+    start, tpl, spec, first, turn, jump, second, rows, mine, got, other, beside, beside2, flat,
+    bank, strain, firsts, turns, mid, mid2, peak, norm, sent, back, wide,
     load_sem, send_sem, recv_sem, side_sem, side_recv,
 ):
     g = lax.axis_index("group")
@@ -85,7 +94,7 @@
         for i, (src, dst) in enumerate(
             [
                 (tpl_hbm, tpl), (spec_hbm, spec), (start_hbm, start),
-                (first_hbm, first), (turn_hbm, turn), (second_hbm, second),
+                (first_hbm, first), (turn_hbm, turn), (jump_hbm, jump), (second_hbm, second),
             ]
         )
     ]
@@ -120,13 +129,6 @@
 
     lax.fori_loop(0, count, fill, 0)
 
-    lag = lax.broadcasted_iota(jnp.int32, (SIDE, 128), 0) + SIDE * (
-        lax.broadcasted_iota(jnp.int32, (SIDE, 128), 1) & (SIDE - 1)
-    )
-    for s in range(SEGS):
-        since = lag - start[s]
-        mask[s] = jnp.where((since >= 0) & (since < VALID), turn[2], 0.0)
-
     got[f] = mine[f]
 
     pl.semaphore_wait(barrier, 2 * count)
@@ -143,12 +145,10 @@
             device_id=(g, to), device_id_type=MESH,
         )
 
-    for o in IN_FAR[:1]:
+    for o in IN_FAR:
         to_far(at(o)).start()
     for o in IN_GROUP:
         to_group(at(o)).start()
-    for o in IN_FAR[1:]:
-        to_far(at(o)).start()
 
     all_group = pltpu.make_async_remote_copy(
         src_ref=mine.at[pl.ds(0, peers)], dst_ref=got.at[pl.ds(0, peers)], send_sem=send_sem.at[0],
@@ -165,6 +165,19 @@
         )
         for i, (src, dst) in enumerate([(got.at[:, 5], beside), (other, beside2)])
     ]
+    def shift(s, carry):
+        begin = start[s]
+        low, high = lax.rem(begin, SIDE), lax.div(begin, SIDE)
+        for q in range(2):
+            firsts[s, SIDE * q:SIDE * (q + 1), :] = first[q, pl.ds(low, SIDE), :].astype(BF16)
+        w0, w1 = turn[0, pl.ds(low, SIDE), :], turn[1, pl.ds(low, SIDE), :]
+        r0, r1 = jump[0, pl.ds(high, 1), :], jump[1, pl.ds(high, 1), :]
+        turns[s, 0] = w0 * r0 - w1 * r1
+        turns[s, 1] = w0 * r1 + w1 * r0
+        return carry
+
+    lax.fori_loop(0, SEGS, shift, 0)
+
     all_group.wait_recv()
     side[0].start()
 
@@ -184,7 +197,7 @@
         bank[p, 0] = re
         bank[p, 1] = im
         total = jnp.sum(re * re + im * im, axis=0, keepdims=True)
-        norm[SEGS * p:SEGS * (p + 1), :] = jnp.broadcast_to(total, (SEGS, 128))
+        norm[8 * p:8 * (p + 1), :] = jnp.broadcast_to(total, (8, 128))
 
     def place(source, home):
         for i in range(ACROSS):
@@ -195,70 +208,62 @@
             strain[4 * home + q, 0] = jnp.where(left, row, turned)
             strain[4 * home + q, 1] = jnp.where(left, turned, row)
 
-    table = first[...]
     table2 = second[...]
-
-    def across(p, homes, dst):
-        h0, h1 = bank[p, 0], bank[p, 1]
-        for n in range(2 * len(homes)):
-            crosses = []
-            for q in range(2):
-                s = 4 * homes[n // 2] + 2 * (n % 2) + q
+    half = lax.rem(g, 2)
+
+    def across(u, low, dst):
+        held = [(bank[2 * u + i, 0], bank[2 * u + i, 1]) for i in range(2)]
+        for q in range(4):
+            for k in range(2):
+                s = low + q + 8 * k
                 d0, d1 = strain[s, 0], strain[s, 1]
-                crosses.append(jnp.concatenate([h0 * d0 + h1 * d1, h0 * d1 - h1 * d0], 0).astype(BF16))
-            y = jnp.dot(table, jnp.concatenate(crosses, 1), preferred_element_type=F32)
-            for q in range(2):
-                re, im = y[:SIDE, 128 * q:128 * (q + 1)], y[SIDE:, 128 * q:128 * (q + 1)]
-                w0, w1 = turn[0], turn[1]
-                dst[2 * n + q, :, 0:128] = (re * w0 - im * w1).astype(BF16)
-                dst[2 * n + q, :, 128:256] = (re * w1 + im * w0).astype(BF16)
-
-    def along(p, homes, src):
-        for n, home in enumerate(homes):
-            z = jnp.dot(src[4 * n:4 * n + 4].reshape(4 * SIDE, 256), table2, preferred_element_type=F32)
+                crosses = [
+                    jnp.concatenate([h0 * d0 + h1 * d1, h0 * d1 - h1 * d0], 0).astype(BF16) for h0, h1 in held
+                ]
+                y = jnp.dot(firsts[s], jnp.concatenate(crosses, 1), preferred_element_type=F32)
+                w0, w1 = turns[s, 0], turns[s, 1]
+                for i in range(2):
+                    re, im = y[:SIDE, 128 * i:128 * (i + 1)], y[SIDE:, 128 * i:128 * (i + 1)]
+                    dst[4 * i + q, :, 256 * k:256 * k + 128] = (re * w0 - im * w1).astype(BF16)
+                    dst[4 * i + q, :, 256 * k + 128:256 * k + 256] = (re * w1 + im * w0).astype(BF16)
+
+    def along(u, low, src):
+        for i in range(2):
+            z = jnp.dot(src[4 * i:4 * i + 4].reshape(4 * SIDE, 512), table2, preferred_element_type=F32)
             for q in range(4):
-                s = 4 * home + q
                 re, im = z[SIDE * q:SIDE * (q + 1), 0:128], z[SIDE * q:SIDE * (q + 1), 128:256]
-                power = (re * re + im * im) * mask[s]
-                peak[pl.ds(SEGS * p + s, 1), :] = jnp.max(power, axis=0, keepdims=True)
-
-    def steps(homes):
+                peak[pl.ds(16 * u + 8 * i + low + q, 1), :] = jnp.max(re * re + im * im, axis=0, keepdims=True)
+
+    def steps(low, one, two):
         def pair(i, carry):
-            across(2 * i + 1, homes, mid2)
-            along(2 * i, homes, mid)
-            across(2 * i + 2, homes, mid)
-            along(2 * i + 1, homes, mid2)
+            across(2 * i + 1, low, two)
+            along(2 * i, low, one)
+            across(2 * i + 2, low, one)
+            along(2 * i + 1, low, two)
             return carry
 
-        lax.fori_loop(0, PAIRS // 2 - 1, pair, 0)
-
-    here, there = (g, far), (near, lax.rem(near + 2, 4))
+        lax.fori_loop(0, 2, pair, 0)
+
+    here, there = 4 * half, 4 - 4 * half
     place(lambda i: got[i, 5], g)
     all_far.wait_recv()
     side[1].start()
     place(lambda i: other[i], far)
     across(0, here, mid)
-    steps(here)
+    steps(here, mid, mid2)
     for copy in side:
         copy.wait_recv()
-    place(lambda i: beside[i], there[0])
-    place(lambda i: beside2[i], there[1])
-    across(PAIRS - 1, here, mid2)
-    along(PAIRS - 2, here, mid)
-    across(0, there, mid)
-    along(PAIRS - 1, here, mid2)
-    steps(there)
-    across(PAIRS - 1, there, mid2)
-    along(PAIRS - 2, there, mid)
-    along(PAIRS - 1, there, mid2)
-
-    def halves(x, fold):
-        return jnp.concatenate([fold(x[:SIDE], axis=0, keepdims=True), fold(x[SIDE:], axis=0, keepdims=True)], 0)
-
-    for j in range(2):
-        best = halves(peak[128 * j:128 * (j + 1), :].T, jnp.max)
-        power = halves(norm[128 * j:128 * (j + 1), :].T, jnp.sum)
-        sent[:, 128 * j:128 * (j + 1)] = best / power
+    place(lambda i: beside[i], near)
+    place(lambda i: beside2[i], lax.rem(near + 2, 4))
+    across(0, there, mid2)
+    along(4, here, mid)
+    steps(there, mid2, mid)
+    along(4, there, mid2)
+    best = (peak[...] * jump[0, 40:41, :]).T
+    power = norm[...].T
+    power = [jnp.sum(power[SIDE * q:SIDE * (q + 1)], axis=0, keepdims=True) for q in range(2)]
+    for k in range(4):
+        sent[k:k + 1, :] = jnp.max(best[32 * k:32 * (k + 1)], axis=0, keepdims=True) / power[k % 2]
     back[f] = sent[...]
 
     def share(to):
@@ -280,39 +285,40 @@
     all_shared.wait_recv()
 
     for i in range(count):
-        for q in range(2):
-            wide[32 * q + i:32 * q + i + 1, :] = back[i, q:q + 1, :]
-    turned = [wide[:, 0:128].T, wide[:, 128:256].T]
-    lane = lax.broadcasted_iota(jnp.int32, (SEGS, 128), 1)
+        for k in range(4):
+            wide[32 * k + i:32 * k + i + 1, :] = back[i, k:k + 1, :]
+    turned = wide[...].T
+    lane = lax.broadcasted_iota(jnp.int32, (8, 128), 1)
     for c in range(5):
-        block = None
-        for k in range(4):
-            j = 4 * c + k
-            q, p = j // PAIRS, j % PAIRS
-            piece = turned[p // 8][SEGS * (p % 8):SEGS * (p % 8 + 1), :]
-            shift = (32 * k - 32 * q) % 128
-            piece = pltpu.roll(piece, shift, 1) if shift else piece
-            block = piece if block is None else jnp.where(lane >= 32 * k, piece, block)
-        out_ref[:, 128 * c:128 * (c + 1)] = block
+        for k in range(2):
+            block = None
+            for n in range(4):
+                q, p = divmod(4 * c + n, PAIRS)
+                piece = turned[8 * p:8 * (p + 1), :]
+                shift = (32 * n - 32 * q - 64 * k) % 128
+                piece = pltpu.roll(piece, shift, 1) if shift else piece
+                block = piece if block is None else jnp.where(lane >= 32 * n, piece, block)
+            out_ref[8 * k:8 * (k + 1), 128 * c:128 * (c + 1)] = block
 
     all_shared.wait_send()
 
 
 def on_device(spectra, templates, valid_start):
-    first, turn, second = tables()
+    first, turn, jump, second = tables()
     anywhere = pl.BlockSpec(memory_space=pl.ANY)
     dma = pltpu.SemaphoreType.DMA
     out = pl.pallas_call(
         kernel,
-        out_shape=jax.ShapeDtypeStruct((SEGS, 640), F32),
-        in_specs=[anywhere] * 6,
+        out_shape=pltpu.VMEM((SEGS, 640), F32),
+        in_specs=[anywhere] * 7,
         out_specs=pl.BlockSpec(memory_space=pltpu.VMEM),
         scratch_shapes=[
             pltpu.SMEM((SEGS,), jnp.int32),
             pltpu.VMEM((64, 2, 640), BF16),
             pltpu.VMEM((2, 4, 64), BF16),
-            pltpu.VMEM(first.shape, BF16),
+            pltpu.VMEM(first.shape, F32),
             pltpu.VMEM(turn.shape, F32),
+            pltpu.VMEM(jump.shape, F32),
             pltpu.VMEM(second.shape, BF16),
             pltpu.VMEM((640, 128), F32),
             pltpu.VMEM((32, 6, 4, 128), BF16),
@@ -323,15 +329,16 @@
             pltpu.VMEM((32 * 24, 128), F32),
             pltpu.VMEM((PAIRS, 2, ACROSS, 128), F32),
             pltpu.VMEM((SEGS, 2, ACROSS, 128), F32),
-            pltpu.VMEM((SEGS, SIDE, 128), F32),
-            pltpu.VMEM((8, SIDE, 256), BF16),
-            pltpu.VMEM((8, SIDE, 256), BF16),
-            pltpu.VMEM((256, 128), F32),
-            pltpu.VMEM((256, 128), F32),
-            pltpu.VMEM((2, 256), F32),
-            pltpu.VMEM((32, 2, 256), F32),
-            pltpu.VMEM((128, 256), F32),
-            dma((6,)),
+            pltpu.VMEM((SEGS, 128, 64), BF16),
+            pltpu.VMEM((SEGS, 2, SIDE, 128), F32),
+            pltpu.VMEM((8, SIDE, 512), BF16),
+            pltpu.VMEM((8, SIDE, 512), BF16),
+            pltpu.VMEM((128, 128), F32),
+            pltpu.VMEM((128, 128), F32),
+            pltpu.VMEM((4, 128), F32),
+            pltpu.VMEM((32, 4, 128), F32),
+            pltpu.VMEM((128, 128), F32),
+            dma((7,)),
             dma((3,)),
             dma((3,)),
             dma((2,)),
@@ -339,8 +346,8 @@
         ],
         compiler_params=pltpu.CompilerParams(collective_id=0, has_side_effects=True),
         name="matched_filter",
-    )(valid_start, templates, jnp.transpose(spectra, (1, 2, 0)), first, turn, second)
-    return jnp.maximum(out, 0.0).T
+    )(valid_start, templates, jnp.transpose(spectra, (1, 2, 0)), first, turn, jump, second)
+    return out.T
 
 
 def solution(mesh):

time: 28.3 us -> 25.8 us (0.912)
  Pallas kernels: 26.7 us -> 25.1 us
  other arithmetic: 1.4 us -> 0 us
  local copies, waits for them, and re-layouts: 0 us -> 0.62 us
    pallas_call x1, Pallas kernels: 26.7 us -> 25.1 us  [on_device(): pl.pallas_call(kernel, out_shape=pltpu.VMEM((SEGS, 640), F32), in_specs=[...]
    transpose x1 -> x0, other arithmetic: 1.4 us -> none  [on_device(): return jnp.maximum(out, 0.0).T]
    unnamed x0 -> x1, local copies, waits for them, and re-layouts: none -> 0.62 us
where the time goes in v3:
time: 25.8 us; the launch traced here: 25.7 us
  Pallas kernels  25.1 us (97%)
  local copies, waits for them, and re-layouts  0.62 us (2%)
    pallas_call x1, Pallas kernels, on_device(): pl.pallas_call(kernel, out_shape=pltpu.VMEM((SEGS, 640), F32), in_specs=[...  25.1 us
    unnamed x1, local copies, waits for them, and re-layouts  0.62 us

profile of v3, /device:TPU:0, one launch (start us, length us, event | category | flops | bytes accessed | tf_op | source)
XLA Modules:
  0.0 25.7 jit_solution(3220658483147395922)
XLA Ops:
  0.0 25.1 %matched_filter.1 = f32[16,640]{1,0:T(8,128)S(1)} custom-call(s32[16]{0:T(128)} %start_hbm.1, bf16[64,2,640]{2,1,0:T(2,128)(2,1)} %tpl_hbm.1, bf16[2,4,64]{2,1,0:T(4,128)(2,1)} %bitcast.3, f32[2,128,64]{2,1,0:T(8,128)} %constant.8.clone.first_hbm, f32[2,128,128]{2,1,0:T(8,128)} %constant.9.clone.turn_hbm, f32[2,48,128]{2,1,0:T(8,128)} %constant.10.clone.jump_hbm, ...), custom_call_target="tpu_custom_call" | custom-call | tf_op jit(solution)/shard_map/matched_filter/pallas_call | solution.py:310
  25.1 0.6 %copy.9 = f32[640,16]{0,1:T(8,128)} copy(f32[640,16]{0,1:T(8,128)S(1)} %bitcast.2) | data formatting | bytes 81920

commit v4 on v3

--- a/solution.py
+++ b/solution.py
@@ -66,14 +66,14 @@
 
 
 IN_GROUP = [o for o in far_first(lambda dy: dy) if o != (0, 0, 0)]
-IN_FAR = far_first(lambda dy: 2 - dy)
+IN_NEAR = far_first(lambda dy: dy)
 
 
 def kernel(
     start_hbm, tpl_hbm, spec_hbm, first_hbm, turn_hbm, jump_hbm, second_hbm, out_ref,
-    start, tpl, spec, first, turn, jump, second, rows, mine, got, other, beside, beside2, flat,
+    start, tpl, spec, first, turn, jump, second, rows, mine, got, other, chunk, beside, beside2, flat,
     bank, strain, firsts, turns, mid, mid2, peak, norm, sent, back, wide,
-    load_sem, send_sem, recv_sem, side_sem, side_recv,
+    load_sem, send_sem, recv_sem,
 ):
     g = lax.axis_index("group")
     f = lax.axis_index("freq")
@@ -102,11 +102,11 @@
         load.start()
 
     barrier = pltpu.get_barrier_semaphore()
-    for o in IN_FAR:
-        pl.semaphore_signal(barrier, inc=1, device_id=(far, at(o)), device_id_type=MESH)
-    for o in IN_GROUP:
-        pl.semaphore_signal(barrier, inc=1, device_id=(g, at(o)), device_id_type=MESH)
-    pl.semaphore_signal(barrier, inc=1, device_id=(near, f), device_id_type=MESH)
+    pl.semaphore_signal(barrier, inc=1, device_id=(far, f), device_id_type=MESH)
+    for o in IN_NEAR:
+        pl.semaphore_signal(barrier, inc=1, device_id=(near, at(o)), device_id_type=MESH)
+        if o in IN_GROUP:
+            pl.semaphore_signal(barrier, inc=1, device_id=(g, at(o)), device_id_type=MESH)
 
     for load in loads:
         load.wait()
@@ -133,38 +133,24 @@
 
     pl.semaphore_wait(barrier, 2 * count)
 
-    def to_far(to):
+    def copy(src, dst, kind, to):
         return pltpu.make_async_remote_copy(
-            src_ref=mine.at[f, 5], dst_ref=other.at[f], send_sem=send_sem.at[1], recv_sem=recv_sem.at[1],
-            device_id=(far, to), device_id_type=MESH,
+            src_ref=src, dst_ref=dst, send_sem=send_sem.at[kind], recv_sem=recv_sem.at[kind],
+            device_id=to, device_id_type=MESH,
         )
 
-    def to_group(to):
-        return pltpu.make_async_remote_copy(
-            src_ref=mine.at[to], dst_ref=got.at[f], send_sem=send_sem.at[0], recv_sem=recv_sem.at[0],
-            device_id=(g, to), device_id_type=MESH,
-        )
-
-    for o in IN_FAR:
-        to_far(at(o)).start()
-    for o in IN_GROUP:
-        to_group(at(o)).start()
-
-    all_group = pltpu.make_async_remote_copy(
-        src_ref=mine.at[pl.ds(0, peers)], dst_ref=got.at[pl.ds(0, peers)], send_sem=send_sem.at[0],
-        recv_sem=recv_sem.at[0], device_id=(near, f), device_id_type=MESH,
-    )
-    all_far = pltpu.make_async_remote_copy(
-        src_ref=other, dst_ref=other, send_sem=send_sem.at[1],
-        recv_sem=recv_sem.at[1], device_id=(near, f), device_id_type=MESH,
-    )
-    side = [
-        pltpu.make_async_remote_copy(
-            src_ref=src, dst_ref=dst, send_sem=side_sem.at[i], recv_sem=side_recv.at[i],
-            device_id=(near, f), device_id_type=MESH,
-        )
-        for i, (src, dst) in enumerate([(got.at[:, 5], beside), (other, beside2)])
-    ]
+    to_far = copy(mine.at[f, 5], chunk, 0, (far, f))
+    to_far.start()
+    for o in IN_NEAR:
+        if o in IN_GROUP:
+            copy(mine.at[at(o)], got.at[f], 1, (g, at(o))).start()
+        copy(mine.at[f, 5], other.at[f], 2, (near, at(o))).start()
+
+    all_group = copy(mine.at[pl.ds(0, peers)], got.at[pl.ds(0, peers)], 1, (near, f))
+    all_near = copy(other, other, 2, (near, f))
+    all_beside = copy(beside.at[pl.ds(0, peers)], beside.at[pl.ds(0, peers)], 3, (near, f))
+    all_beside2 = copy(beside2, beside2, 4, (near, f))
+    all_shared = copy(back.at[pl.ds(0, peers)], back.at[pl.ds(0, peers)], 5, (near, f))
     def shift(s, carry):
         begin = start[s]
         low, high = lax.rem(begin, SIDE), lax.div(begin, SIDE)
@@ -178,8 +164,14 @@
 
     lax.fori_loop(0, SEGS, shift, 0)
 
+    to_far.wait_recv()
+    for o in IN_NEAR:
+        if o in IN_GROUP:
+            copy(chunk, beside.at[f], 3, (g, at(o))).start()
+        copy(chunk, beside2.at[f], 4, (near, at(o))).start()
+    beside[f] = chunk[...]
+
     all_group.wait_recv()
-    side[0].start()
 
     left = lax.broadcasted_iota(jnp.int32, (ACROSS, 128), 1) < SIDE
 
@@ -209,13 +201,13 @@
             strain[4 * home + q, 1] = jnp.where(left, turned, row)
 
     table2 = second[...]
-    half = lax.rem(g, 2)
+    half = g // 2
 
     def across(u, low, dst):
         held = [(bank[2 * u + i, 0], bank[2 * u + i, 1]) for i in range(2)]
         for q in range(4):
             for k in range(2):
-                s = low + q + 8 * k
+                s = 2 * low + q + 4 * k
                 d0, d1 = strain[s, 0], strain[s, 1]
                 crosses = [
                     jnp.concatenate([h0 * d0 + h1 * d1, h0 * d1 - h1 * d0], 0).astype(BF16) for h0, h1 in held
@@ -246,14 +238,13 @@
 
     here, there = 4 * half, 4 - 4 * half
     place(lambda i: got[i, 5], g)
-    all_far.wait_recv()
-    side[1].start()
-    place(lambda i: other[i], far)
+    all_near.wait_recv()
+    place(lambda i: other[i], near)
     across(0, here, mid)
     steps(here, mid, mid2)
-    for copy in side:
-        copy.wait_recv()
-    place(lambda i: beside[i], near)
+    all_beside.wait_recv()
+    all_beside2.wait_recv()
+    place(lambda i: beside[i], far)
     place(lambda i: beside2[i], lax.rem(near + 2, 4))
     across(0, there, mid2)
     along(4, here, mid)
@@ -266,22 +257,10 @@
         sent[k:k + 1, :] = jnp.max(best[32 * k:32 * (k + 1)], axis=0, keepdims=True) / power[k % 2]
     back[f] = sent[...]
 
-    def share(to):
-        return pltpu.make_async_remote_copy(
-            src_ref=sent, dst_ref=back.at[f], send_sem=send_sem.at[2], recv_sem=recv_sem.at[2],
-            device_id=(g, to), device_id_type=MESH,
-        )
-
     for o in IN_GROUP:
-        share(at(o)).start()
-    all_group.wait_send()
-    all_far.wait_send()
-    for copy in side:
-        copy.wait_send()
-    all_shared = pltpu.make_async_remote_copy(
-        src_ref=back.at[pl.ds(0, peers)], dst_ref=back.at[pl.ds(0, peers)], send_sem=send_sem.at[2],
-        recv_sem=recv_sem.at[2], device_id=(near, f), device_id_type=MESH,
-    )
+        copy(sent, back.at[f], 5, (g, at(o))).start()
+    for whole in (to_far, all_group, all_near, all_beside, all_beside2):
+        whole.wait_send()
     all_shared.wait_recv()
 
     for i in range(count):
@@ -289,7 +268,9 @@
             wide[32 * k + i:32 * k + i + 1, :] = back[i, k:k + 1, :]
     turned = wide[...].T
     lane = lax.broadcasted_iota(jnp.int32, (8, 128), 1)
+    upper = lax.broadcasted_iota(jnp.int32, (8, 128), 0) < 4
     for c in range(5):
+        blocks = []
         for k in range(2):
             block = None
             for n in range(4):
@@ -298,7 +279,10 @@
                 shift = (32 * n - 32 * q - 64 * k) % 128
                 piece = pltpu.roll(piece, shift, 1) if shift else piece
                 block = piece if block is None else jnp.where(lane >= 32 * n, piece, block)
-            out_ref[8 * k:8 * (k + 1), 128 * c:128 * (c + 1)] = block
+            blocks.append(block)
+        one, two = blocks
+        out_ref[0:8, 128 * c:128 * (c + 1)] = jnp.where(upper, one, pltpu.roll(two, 4, 0))
+        out_ref[8:16, 128 * c:128 * (c + 1)] = jnp.where(upper, pltpu.roll(one, 4, 0), two)
 
     all_shared.wait_send()
 
@@ -324,6 +308,7 @@
             pltpu.VMEM((32, 6, 4, 128), BF16),
             pltpu.VMEM((32, 6, 4, 128), BF16),
             pltpu.VMEM((32, 4, 128), BF16),
+            pltpu.VMEM((4, 128), BF16),
             pltpu.VMEM((32, 4, 128), BF16),
             pltpu.VMEM((32, 4, 128), BF16),
             pltpu.VMEM((32 * 24, 128), F32),
@@ -339,10 +324,8 @@
             pltpu.VMEM((32, 4, 128), F32),
             pltpu.VMEM((128, 128), F32),
             dma((7,)),
-            dma((3,)),
-            dma((3,)),
-            dma((2,)),
-            dma((2,)),
+            dma((6,)),
+            dma((6,)),
         ],
         compiler_params=pltpu.CompilerParams(collective_id=0, has_side_effects=True),
         name="matched_filter",

time: 25.8 us -> 26.7 us (1.035)
  the two profiles are of different devices: /device:TPU:0 before, /device:TPU:1 now
where the time goes in v4:
time: 26.7 us; the launch traced here: 26.5 us
  Pallas kernels  25.9 us (97%)
  local copies, waits for them, and re-layouts  0.62 us (2%)
    pallas_call x1, Pallas kernels, on_device(): pl.pallas_call(kernel, out_shape=pltpu.VMEM((SEGS, 640), F32), in_specs=[...  25.9 us
    unnamed x1, local copies, waits for them, and re-layouts  0.62 us

profile of v4, /device:TPU:1, one launch (start us, length us, event | category | flops | bytes accessed | tf_op | source)
XLA Modules:
  0.0 26.5 jit_solution(14512202115028499321)
XLA Ops:
  0.0 25.9 %matched_filter.1 = f32[16,640]{1,0:T(8,128)S(1)} custom-call(s32[16]{0:T(128)} %start_hbm.1, bf16[64,2,640]{2,1,0:T(2,128)(2,1)} %tpl_hbm.1, bf16[2,4,64]{2,1,0:T(4,128)(2,1)} %bitcast.3, f32[2,128,64]{2,1,0:T(8,128)} %constant.8.clone.first_hbm, f32[2,128,128]{2,1,0:T(8,128)} %constant.9.clone.turn_hbm, f32[2,48,128]{2,1,0:T(8,128)} %constant.10.clone.jump_hbm, ...), custom_call_target="tpu_custom_call" | custom-call | tf_op jit(solution)/shard_map/matched_filter/pallas_call | solution.py:294
  25.9 0.6 %copy.9 = f32[640,16]{0,1:T(8,128)} copy(f32[640,16]{0,1:T(8,128)S(1)} %bitcast.2) | data formatting | bytes 81920

commit v5 on v4

--- a/solution.py
+++ b/solution.py
@@ -67,6 +67,7 @@
 
 IN_GROUP = [o for o in far_first(lambda dy: dy) if o != (0, 0, 0)]
 IN_NEAR = far_first(lambda dy: dy)
+IN_FAR = far_first(lambda dy: 2 - dy)
 
 
 def kernel(
@@ -102,11 +103,21 @@
         load.start()
 
     barrier = pltpu.get_barrier_semaphore()
+    across_g = lax.rem(near + 2, 4)
+    late = g // 2
     pl.semaphore_signal(barrier, inc=1, device_id=(far, f), device_id_type=MESH)
     for o in IN_NEAR:
         pl.semaphore_signal(barrier, inc=1, device_id=(near, at(o)), device_id_type=MESH)
         if o in IN_GROUP:
             pl.semaphore_signal(barrier, inc=1, device_id=(g, at(o)), device_id_type=MESH)
+
+    @pl.when(late == 0)
+    def _():
+        for o in IN_FAR:
+            pl.semaphore_signal(barrier, inc=1, device_id=(across_g, at(o)), device_id_type=MESH)
+            if o != (0, 0, 0):
+                pl.semaphore_signal(barrier, inc=1, device_id=(far, at(o)), device_id_type=MESH)
+
 
     for load in loads:
         load.wait()
@@ -131,7 +142,7 @@
 
     got[f] = mine[f]
 
-    pl.semaphore_wait(barrier, 2 * count)
+    pl.semaphore_wait(barrier, 2 * count + (2 * count - 1) * late)
 
     def copy(src, dst, kind, to):
         return pltpu.make_async_remote_copy(
@@ -139,16 +150,28 @@
             device_id=to, device_id_type=MESH,
         )
 
-    to_far = copy(mine.at[f, 5], chunk, 0, (far, f))
-    to_far.start()
+    own_chunk = mine.at[f, 5]
+    to_far = copy(own_chunk, chunk, 0, (far, f))
+
+    @pl.when(late == 0)
+    def _():
+        to_far.start()
+
+    @pl.when(late == 1)
+    def _():
+        for o in IN_FAR:
+            copy(own_chunk, beside.at[f], 3, (far, at(o))).start()
+            copy(own_chunk, beside2.at[f], 4, (across_g, at(o))).start()
+
     for o in IN_NEAR:
         if o in IN_GROUP:
             copy(mine.at[at(o)], got.at[f], 1, (g, at(o))).start()
-        copy(mine.at[f, 5], other.at[f], 2, (near, at(o))).start()
+        copy(own_chunk, other.at[f], 2, (near, at(o))).start()
 
     all_group = copy(mine.at[pl.ds(0, peers)], got.at[pl.ds(0, peers)], 1, (near, f))
     all_near = copy(other, other, 2, (near, f))
-    all_beside = copy(beside.at[pl.ds(0, peers)], beside.at[pl.ds(0, peers)], 3, (near, f))
+    all_beside = copy(beside, beside, 3, (near, f))
+    most_beside = copy(beside.at[pl.ds(0, peers)], beside.at[pl.ds(0, peers)], 3, (near, f))
     all_beside2 = copy(beside2, beside2, 4, (near, f))
     all_shared = copy(back.at[pl.ds(0, peers)], back.at[pl.ds(0, peers)], 5, (near, f))
     def shift(s, carry):
@@ -164,12 +187,14 @@
 
     lax.fori_loop(0, SEGS, shift, 0)
 
-    to_far.wait_recv()
-    for o in IN_NEAR:
-        if o in IN_GROUP:
-            copy(chunk, beside.at[f], 3, (g, at(o))).start()
-        copy(chunk, beside2.at[f], 4, (near, at(o))).start()
-    beside[f] = chunk[...]
+    @pl.when(late == 1)
+    def _():
+        to_far.wait_recv()
+        for o in IN_NEAR:
+            if o in IN_GROUP:
+                copy(chunk, beside.at[f], 3, (g, at(o))).start()
+            copy(chunk, beside2.at[f], 4, (near, at(o))).start()
+        beside[f] = chunk[...]
 
     all_group.wait_recv()
 
@@ -242,10 +267,17 @@
     place(lambda i: other[i], near)
     across(0, here, mid)
     steps(here, mid, mid2)
-    all_beside.wait_recv()
+    @pl.when(late == 0)
+    def _():
+        all_beside.wait_recv()
+
+    @pl.when(late == 1)
+    def _():
+        most_beside.wait_recv()
+
     all_beside2.wait_recv()
     place(lambda i: beside[i], far)
-    place(lambda i: beside2[i], lax.rem(near + 2, 4))
+    place(lambda i: beside2[i], across_g)
     across(0, there, mid2)
     along(4, here, mid)
     steps(there, mid2, mid)
@@ -259,8 +291,18 @@
 
     for o in IN_GROUP:
         copy(sent, back.at[f], 5, (g, at(o))).start()
-    for whole in (to_far, all_group, all_near, all_beside, all_beside2):
-        whole.wait_send()
+    all_group.wait_send()
+    all_near.wait_send()
+
+    @pl.when(late == 0)
+    def _():
+        to_far.wait_send()
+
+    @pl.when(late == 1)
+    def _():
+        for whole in (all_beside, most_beside, all_beside2, all_beside2):
+            whole.wait_send()
+
     all_shared.wait_recv()
 
     for i in range(count):

time: 26.7 us -> 25.9 us (0.970)
  the two profiles are of different devices: /device:TPU:1 before, /device:TPU:16 now
where the time goes in v5:
time: 25.9 us; the launch traced here: 25.7 us
  Pallas kernels  25.1 us (97%)
  local copies, waits for them, and re-layouts  0.62 us (2%)
    pallas_call x1, Pallas kernels, on_device(): pl.pallas_call(kernel, out_shape=pltpu.VMEM((SEGS, 640), F32), in_specs=[...  25.1 us
    unnamed x1, local copies, waits for them, and re-layouts  0.62 us

profile of v5, /device:TPU:16, one launch (start us, length us, event | category | flops | bytes accessed | tf_op | source)
XLA Modules:
  0.0 25.7 jit_solution(8350119179382828452)
XLA Ops:
  0.0 25.1 %matched_filter.1 = f32[16,640]{1,0:T(8,128)S(1)} custom-call(s32[16]{0:T(128)} %start_hbm.1, bf16[64,2,640]{2,1,0:T(2,128)(2,1)} %tpl_hbm.1, bf16[2,4,64]{2,1,0:T(4,128)(2,1)} %bitcast.3, f32[2,128,64]{2,1,0:T(8,128)} %constant.8.clone.first_hbm, f32[2,128,128]{2,1,0:T(8,128)} %constant.9.clone.turn_hbm, f32[2,48,128]{2,1,0:T(8,128)} %constant.10.clone.jump_hbm, ...), custom_call_target="tpu_custom_call" | custom-call | tf_op jit(solution)/shard_map/matched_filter/pallas_call | solution.py:336
  25.1 0.6 %copy.9 = f32[640,16]{0,1:T(8,128)} copy(f32[640,16]{0,1:T(8,128)S(1)} %bitcast.2) | data formatting | bytes 81920

commit v6 on v5

--- a/solution.py
+++ b/solution.py
@@ -60,14 +60,17 @@
     return jnp.asarray(first, F32), jnp.asarray(turn, F32), jnp.asarray(jump, F32), jnp.asarray(second, BF16)
 
 
-def far_first(distance):
+def far_first(kinds):
+    def hops(entry):
+        (kind, (dz, dx, dy)) = entry
+        return min(dz, 4 - dz) + min(dx, 4 - dx) + (2 - dy if kind in (FAR, BEYOND) else dy)
+
     offsets = [(dz, dx, dy) for dz in range(4) for dx in range(4) for dy in range(2)]
-    return sorted(offsets, key=lambda o: -(min(o[0], 4 - o[0]) + min(o[1], 4 - o[1]) + distance(o[2])))
-
-
-IN_GROUP = [o for o in far_first(lambda dy: dy) if o != (0, 0, 0)]
-IN_NEAR = far_first(lambda dy: dy)
-IN_FAR = far_first(lambda dy: 2 - dy)
+    entries = [(kind, o) for o in offsets for kind in kinds if (kind, o) != (GROUP, (0, 0, 0))]
+    return sorted(entries, key=lambda entry: (-hops(entry), kinds.index(entry[0])))
+
+
+GROUP, NEAR, FAR, BEYOND = range(4)
 
 
 def kernel(
@@ -105,19 +108,16 @@
     barrier = pltpu.get_barrier_semaphore()
     across_g = lax.rem(near + 2, 4)
     late = g // 2
+    group_of = (g, near, far, across_g)
     pl.semaphore_signal(barrier, inc=1, device_id=(far, f), device_id_type=MESH)
-    for o in IN_NEAR:
-        pl.semaphore_signal(barrier, inc=1, device_id=(near, at(o)), device_id_type=MESH)
-        if o in IN_GROUP:
-            pl.semaphore_signal(barrier, inc=1, device_id=(g, at(o)), device_id_type=MESH)
+    for kind, o in far_first((GROUP, NEAR)):
+        pl.semaphore_signal(barrier, inc=1, device_id=(group_of[kind], at(o)), device_id_type=MESH)
 
     @pl.when(late == 0)
     def _():
-        for o in IN_FAR:
-            pl.semaphore_signal(barrier, inc=1, device_id=(across_g, at(o)), device_id_type=MESH)
-            if o != (0, 0, 0):
-                pl.semaphore_signal(barrier, inc=1, device_id=(far, at(o)), device_id_type=MESH)
-
+        for kind, o in far_first((FAR, BEYOND)):
+            if (kind, o) != (FAR, (0, 0, 0)):
+                pl.semaphore_signal(barrier, inc=1, device_id=(group_of[kind], at(o)), device_id_type=MESH)
 
     for load in loads:
         load.wait()
@@ -153,20 +153,21 @@
     own_chunk = mine.at[f, 5]
     to_far = copy(own_chunk, chunk, 0, (far, f))
 
+    def give(kind, to):
+        if kind == GROUP:
+            return copy(mine.at[to], got.at[f], 1, (g, to))
+        return copy(own_chunk, (other, beside, beside2)[kind - 1].at[f], kind + 1, (group_of[kind], to))
+
     @pl.when(late == 0)
     def _():
         to_far.start()
+        for kind, o in far_first((GROUP, NEAR)):
+            give(kind, at(o)).start()
 
     @pl.when(late == 1)
     def _():
-        for o in IN_FAR:
-            copy(own_chunk, beside.at[f], 3, (far, at(o))).start()
-            copy(own_chunk, beside2.at[f], 4, (across_g, at(o))).start()
-
-    for o in IN_NEAR:
-        if o in IN_GROUP:
-            copy(mine.at[at(o)], got.at[f], 1, (g, at(o))).start()
-        copy(own_chunk, other.at[f], 2, (near, at(o))).start()
+        for kind, o in far_first((GROUP, NEAR, FAR, BEYOND)):
+            give(kind, at(o)).start()
 
     all_group = copy(mine.at[pl.ds(0, peers)], got.at[pl.ds(0, peers)], 1, (near, f))
     all_near = copy(other, other, 2, (near, f))
@@ -190,10 +191,8 @@
     @pl.when(late == 1)
     def _():
         to_far.wait_recv()
-        for o in IN_NEAR:
-            if o in IN_GROUP:
-                copy(chunk, beside.at[f], 3, (g, at(o))).start()
-            copy(chunk, beside2.at[f], 4, (near, at(o))).start()
+        for kind, o in far_first((GROUP, NEAR)):
+            copy(chunk, (beside, beside2)[kind].at[f], 3 + kind, (group_of[kind], at(o))).start()
         beside[f] = chunk[...]
 
     all_group.wait_recv()
@@ -252,14 +251,11 @@
                 peak[pl.ds(16 * u + 8 * i + low + q, 1), :] = jnp.max(re * re + im * im, axis=0, keepdims=True)
 
     def steps(low, one, two):
-        def pair(i, carry):
+        for i in range(2):
             across(2 * i + 1, low, two)
             along(2 * i, low, one)
             across(2 * i + 2, low, one)
             along(2 * i + 1, low, two)
-            return carry
-
-        lax.fori_loop(0, 2, pair, 0)
 
     here, there = 4 * half, 4 - 4 * half
     place(lambda i: got[i, 5], g)
@@ -289,7 +285,7 @@
         sent[k:k + 1, :] = jnp.max(best[32 * k:32 * (k + 1)], axis=0, keepdims=True) / power[k % 2]
     back[f] = sent[...]
 
-    for o in IN_GROUP:
+    for _, o in far_first((GROUP,)):
         copy(sent, back.at[f], 5, (g, at(o))).start()
     all_group.wait_send()
     all_near.wait_send()

time: 25.9 us -> 25.1 us (0.969)
  Pallas kernels: 25.1 us -> 24.3 us
    pallas_call x1, Pallas kernels: 25.1 us -> 24.3 us  [on_device(): pl.pallas_call(kernel, out_shape=pltpu.VMEM((SEGS, 640), F32), in_specs=[...]
where the time goes in v6:
time: 25.1 us; the launch traced here: 25 us
  Pallas kernels  24.3 us (97%)
  local copies, waits for them, and re-layouts  0.62 us (2%)
    pallas_call x1, Pallas kernels, on_device(): pl.pallas_call(kernel, out_shape=pltpu.VMEM((SEGS, 640), F32), in_specs=[...  24.3 us
    unnamed x1, local copies, waits for them, and re-layouts  0.62 us

profile of v6, /device:TPU:16, one launch (start us, length us, event | category | flops | bytes accessed | tf_op | source)
XLA Modules:
  0.0 25.0 jit_solution(15855616304433687317)
XLA Ops:
  0.0 24.3 %matched_filter.1 = f32[16,640]{1,0:T(8,128)S(1)} custom-call(s32[16]{0:T(128)} %start_hbm.1, bf16[64,2,640]{2,1,0:T(2,128)(2,1)} %tpl_hbm.1, bf16[2,4,64]{2,1,0:T(4,128)(2,1)} %bitcast.3, f32[2,128,64]{2,1,0:T(8,128)} %constant.8.clone.first_hbm, f32[2,128,128]{2,1,0:T(8,128)} %constant.9.clone.turn_hbm, f32[2,48,128]{2,1,0:T(8,128)} %constant.10.clone.jump_hbm, ...), custom_call_target="tpu_custom_call" | custom-call | tf_op jit(solution)/shard_map/matched_filter/pallas_call | solution.py:332
  24.3 0.6 %copy.9 = f32[640,16]{0,1:T(8,128)} copy(f32[640,16]{0,1:T(8,128)S(1)} %bitcast.2) | data formatting | bytes 81920

commit v7 on v6

--- a/solution.py
+++ b/solution.py
@@ -63,14 +63,14 @@
 def far_first(kinds):
     def hops(entry):
         (kind, (dz, dx, dy)) = entry
-        return min(dz, 4 - dz) + min(dx, 4 - dx) + (2 - dy if kind in (FAR, BEYOND) else dy)
+        return min(dz, 4 - dz) + min(dx, 4 - dx) + (2 - dy if kind == FAR else dy)
 
     offsets = [(dz, dx, dy) for dz in range(4) for dx in range(4) for dy in range(2)]
     entries = [(kind, o) for o in offsets for kind in kinds if (kind, o) != (GROUP, (0, 0, 0))]
     return sorted(entries, key=lambda entry: (-hops(entry), kinds.index(entry[0])))
 
 
-GROUP, NEAR, FAR, BEYOND = range(4)
+GROUP, FAR = range(2)
 
 
 def kernel(
@@ -108,16 +108,17 @@
     barrier = pltpu.get_barrier_semaphore()
     across_g = lax.rem(near + 2, 4)
     late = g // 2
-    group_of = (g, near, far, across_g)
+    group_of = (g, far)
     pl.semaphore_signal(barrier, inc=1, device_id=(far, f), device_id_type=MESH)
-    for kind, o in far_first((GROUP, NEAR)):
-        pl.semaphore_signal(barrier, inc=1, device_id=(group_of[kind], at(o)), device_id_type=MESH)
+    for _, o in far_first((GROUP,)):
+        pl.semaphore_signal(barrier, inc=1, device_id=(g, at(o)), device_id_type=MESH)
+    pl.semaphore_signal(barrier, inc=1, device_id=(near, f), device_id_type=MESH)
 
     @pl.when(late == 0)
     def _():
-        for kind, o in far_first((FAR, BEYOND)):
-            if (kind, o) != (FAR, (0, 0, 0)):
-                pl.semaphore_signal(barrier, inc=1, device_id=(group_of[kind], at(o)), device_id_type=MESH)
+        for _, o in far_first((FAR,)):
+            if o != (0, 0, 0):
+                pl.semaphore_signal(barrier, inc=1, device_id=(far, at(o)), device_id_type=MESH)
 
     for load in loads:
         load.wait()
@@ -142,7 +143,7 @@
 
     got[f] = mine[f]
 
-    pl.semaphore_wait(barrier, 2 * count + (2 * count - 1) * late)
+    pl.semaphore_wait(barrier, count + 1 + peers * late)
 
     def copy(src, dst, kind, to):
         return pltpu.make_async_remote_copy(
@@ -156,25 +157,26 @@
     def give(kind, to):
         if kind == GROUP:
             return copy(mine.at[to], got.at[f], 1, (g, to))
-        return copy(own_chunk, (other, beside, beside2)[kind - 1].at[f], kind + 1, (group_of[kind], to))
+        return copy(own_chunk, beside.at[f], 3, (far, to))
 
     @pl.when(late == 0)
     def _():
         to_far.start()
-        for kind, o in far_first((GROUP, NEAR)):
+        for kind, o in far_first((GROUP,)):
             give(kind, at(o)).start()
 
     @pl.when(late == 1)
     def _():
-        for kind, o in far_first((GROUP, NEAR, FAR, BEYOND)):
+        for kind, o in far_first((GROUP, FAR)):
             give(kind, at(o)).start()
 
     all_group = copy(mine.at[pl.ds(0, peers)], got.at[pl.ds(0, peers)], 1, (near, f))
-    all_near = copy(other, other, 2, (near, f))
     all_beside = copy(beside, beside, 3, (near, f))
     most_beside = copy(beside.at[pl.ds(0, peers)], beside.at[pl.ds(0, peers)], 3, (near, f))
-    all_beside2 = copy(beside2, beside2, 4, (near, f))
     all_shared = copy(back.at[pl.ds(0, peers)], back.at[pl.ds(0, peers)], 5, (near, f))
+    own_over = copy(got.at[:, 5], other, 2, (near, f))
+    far_over = copy(beside, beside2, 4, (near, f))
+
     def shift(s, carry):
         begin = start[s]
         low, high = lax.rem(begin, SIDE), lax.div(begin, SIDE)
@@ -191,11 +193,12 @@
     @pl.when(late == 1)
     def _():
         to_far.wait_recv()
-        for kind, o in far_first((GROUP, NEAR)):
-            copy(chunk, (beside, beside2)[kind].at[f], 3 + kind, (group_of[kind], at(o))).start()
+        for _, o in far_first((GROUP,)):
+            copy(chunk, beside.at[f], 3, (g, at(o))).start()
         beside[f] = chunk[...]
 
     all_group.wait_recv()
+    own_over.start()
 
     left = lax.broadcasted_iota(jnp.int32, (ACROSS, 128), 1) < SIDE
 
@@ -225,13 +228,12 @@
             strain[4 * home + q, 1] = jnp.where(left, turned, row)
 
     table2 = second[...]
-    half = g // 2
-
-    def across(u, low, dst):
+
+    def across(u, home, dst):
         held = [(bank[2 * u + i, 0], bank[2 * u + i, 1]) for i in range(2)]
-        for q in range(4):
+        for q in range(2):
             for k in range(2):
-                s = 2 * low + q + 4 * k
+                s = 4 * home + q + 2 * k
                 d0, d1 = strain[s, 0], strain[s, 1]
                 crosses = [
                     jnp.concatenate([h0 * d0 + h1 * d1, h0 * d1 - h1 * d0], 0).astype(BF16) for h0, h1 in held
@@ -240,44 +242,49 @@
                 w0, w1 = turns[s, 0], turns[s, 1]
                 for i in range(2):
                     re, im = y[:SIDE, 128 * i:128 * (i + 1)], y[SIDE:, 128 * i:128 * (i + 1)]
-                    dst[4 * i + q, :, 256 * k:256 * k + 128] = (re * w0 - im * w1).astype(BF16)
-                    dst[4 * i + q, :, 256 * k + 128:256 * k + 256] = (re * w1 + im * w0).astype(BF16)
-
-    def along(u, low, src):
-        for i in range(2):
-            z = jnp.dot(src[4 * i:4 * i + 4].reshape(4 * SIDE, 512), table2, preferred_element_type=F32)
-            for q in range(4):
-                re, im = z[SIDE * q:SIDE * (q + 1), 0:128], z[SIDE * q:SIDE * (q + 1), 128:256]
-                peak[pl.ds(16 * u + 8 * i + low + q, 1), :] = jnp.max(re * re + im * im, axis=0, keepdims=True)
-
-    def steps(low, one, two):
-        for i in range(2):
-            across(2 * i + 1, low, two)
-            along(2 * i, low, one)
-            across(2 * i + 2, low, one)
-            along(2 * i + 1, low, two)
-
-    here, there = 4 * half, 4 - 4 * half
-    place(lambda i: got[i, 5], g)
-    all_near.wait_recv()
-    place(lambda i: other[i], near)
-    across(0, here, mid)
-    steps(here, mid, mid2)
-    @pl.when(late == 0)
-    def _():
-        all_beside.wait_recv()
-
-    @pl.when(late == 1)
-    def _():
-        most_beside.wait_recv()
-
-    all_beside2.wait_recv()
-    place(lambda i: beside[i], far)
-    place(lambda i: beside2[i], across_g)
-    across(0, there, mid2)
-    along(4, here, mid)
-    steps(there, mid2, mid)
-    along(4, there, mid2)
+                    dst[2 * i + q, :, 256 * k:256 * k + 128] = (re * w0 - im * w1).astype(BF16)
+                    dst[2 * i + q, :, 256 * k + 128:256 * k + 256] = (re * w1 + im * w0).astype(BF16)
+
+    def along(u, home, src):
+        z = jnp.dot(src[...].reshape(4 * SIDE, 512), table2, preferred_element_type=F32)
+        for n in range(4):
+            re, im = z[SIDE * n:SIDE * (n + 1), 0:128], z[SIDE * n:SIDE * (n + 1), 128:256]
+            row = 16 * u + 8 * (n // 2) + 2 * home + n % 2
+            peak[pl.ds(row, 1), :] = jnp.max(re * re + im * im, axis=0, keepdims=True)
+
+    homes = (g, near, far, across_g)
+    parts = (lambda i: got[i, 5], lambda i: other[i], lambda i: beside[i], lambda i: beside2[i])
+
+    def arrive(n):
+        if n == 1:
+            own_over.wait_recv()
+        if n == 2:
+            @pl.when(late == 0)
+            def _():
+                all_beside.wait_recv()
+
+            @pl.when(late == 1)
+            def _():
+                most_beside.wait_recv()
+
+            far_over.start()
+        if n == 3:
+            far_over.wait_recv()
+
+    steps = [(u, home) for home in range(4) for u in range(PAIRS // 2)]
+    mids = (mid, mid2)
+    for n, (u, home) in enumerate(steps):
+        if u == 0:
+
+            arrive(home)
+
+            place(parts[home], homes[home])
+
+        across(u, homes[home], mids[n % 2])
+        if n > 0:
+            along(steps[n - 1][0], homes[steps[n - 1][1]], mids[(n - 1) % 2])
+    along(steps[-1][0], homes[-1], mids[(len(steps) - 1) % 2])
+
     best = (peak[...] * jump[0, 40:41, :]).T
     power = norm[...].T
     power = [jnp.sum(power[SIDE * q:SIDE * (q + 1)], axis=0, keepdims=True) for q in range(2)]
@@ -287,8 +294,8 @@
 
     for _, o in far_first((GROUP,)):
         copy(sent, back.at[f], 5, (g, at(o))).start()
-    all_group.wait_send()
-    all_near.wait_send()
+    for whole in (all_group, own_over, far_over):
+        whole.wait_send()
 
     @pl.when(late == 0)
     def _():
@@ -296,8 +303,8 @@
 
     @pl.when(late == 1)
     def _():
-        for whole in (all_beside, most_beside, all_beside2, all_beside2):
-            whole.wait_send()
+        all_beside.wait_send()
+        most_beside.wait_send()
 
     all_shared.wait_recv()
 
@@ -306,7 +313,7 @@
             wide[32 * k + i:32 * k + i + 1, :] = back[i, k:k + 1, :]
     turned = wide[...].T
     lane = lax.broadcasted_iota(jnp.int32, (8, 128), 1)
-    upper = lax.broadcasted_iota(jnp.int32, (8, 128), 0) < 4
+    row = lax.broadcasted_iota(jnp.int32, (8, 128), 0)
     for c in range(5):
         blocks = []
         for k in range(2):
@@ -319,8 +326,11 @@
                 block = piece if block is None else jnp.where(lane >= 32 * n, piece, block)
             blocks.append(block)
         one, two = blocks
-        out_ref[0:8, 128 * c:128 * (c + 1)] = jnp.where(upper, one, pltpu.roll(two, 4, 0))
-        out_ref[8:16, 128 * c:128 * (c + 1)] = jnp.where(upper, pltpu.roll(one, 4, 0), two)
+        for n, shifts in enumerate(((0, 2, 2, 4), (4, 6, 6, 0))):
+            moved = [pltpu.roll(x, d, 0) if d else x for x, d in zip((one, two, one, two), shifts)]
+            low = jnp.where(row < 2, moved[0], moved[1])
+            high = jnp.where(row < 6, moved[2], moved[3])
+            out_ref[8 * n:8 * (n + 1), 128 * c:128 * (c + 1)] = jnp.where(row < 4, low, high)
 
     all_shared.wait_send()
 
@@ -354,8 +364,8 @@
             pltpu.VMEM((SEGS, 2, ACROSS, 128), F32),
             pltpu.VMEM((SEGS, 128, 64), BF16),
             pltpu.VMEM((SEGS, 2, SIDE, 128), F32),
-            pltpu.VMEM((8, SIDE, 512), BF16),
-            pltpu.VMEM((8, SIDE, 512), BF16),
+            pltpu.VMEM((4, SIDE, 512), BF16),
+            pltpu.VMEM((4, SIDE, 512), BF16),
             pltpu.VMEM((128, 128), F32),
             pltpu.VMEM((128, 128), F32),
             pltpu.VMEM((4, 128), F32),

time: 25.1 us -> 23.8 us (0.948)
  Pallas kernels: 24.3 us -> 23 us
    pallas_call x1, Pallas kernels: 24.3 us -> 23 us  [on_device(): pl.pallas_call(kernel, out_shape=pltpu.VMEM((SEGS, 640), F32), in_specs=[...]
where the time goes in v7:
time: 23.8 us; the launch traced here: 23.6 us
  Pallas kernels  23 us (97%)
  local copies, waits for them, and re-layouts  0.62 us (3%)
    pallas_call x1, Pallas kernels, on_device(): pl.pallas_call(kernel, out_shape=pltpu.VMEM((SEGS, 640), F32), in_specs=[...  23 us
    unnamed x1, local copies, waits for them, and re-layouts  0.62 us

profile of v7, /device:TPU:16, one launch (start us, length us, event | category | flops | bytes accessed | tf_op | source)
XLA Modules:
  0.0 23.6 jit_solution(6600552778882368012)
XLA Ops:
  0.0 23.0 %matched_filter.1 = f32[16,640]{1,0:T(8,128)S(1)} custom-call(s32[16]{0:T(128)} %start_hbm.1, bf16[64,2,640]{2,1,0:T(2,128)(2,1)} %tpl_hbm.1, bf16[2,4,64]{2,1,0:T(4,128)(2,1)} %bitcast.3, f32[2,128,64]{2,1,0:T(8,128)} %constant.8.clone.first_hbm, f32[2,128,128]{2,1,0:T(8,128)} %constant.9.clone.turn_hbm, f32[2,48,128]{2,1,0:T(8,128)} %constant.10.clone.jump_hbm, ...), custom_call_target="tpu_custom_call" | custom-call | tf_op jit(solution)/shard_map/matched_filter/pallas_call | solution.py:342
  23.0 0.6 %copy.9 = f32[640,16]{0,1:T(8,128)} copy(f32[640,16]{0,1:T(8,128)S(1)} %bitcast.2) | data formatting | bytes 81920

commit v8 on v7

--- a/solution.py
+++ b/solution.py
@@ -75,8 +75,8 @@
 
 def kernel(
     start_hbm, tpl_hbm, spec_hbm, first_hbm, turn_hbm, jump_hbm, second_hbm, out_ref,
-    start, tpl, spec, first, turn, jump, second, rows, mine, got, other, chunk, beside, beside2, flat,
-    bank, strain, firsts, turns, mid, mid2, peak, norm, sent, back, wide,
+    start, tpl, spec, first, turn, jump, second, rows, mine, got, other, chunk, beside, beside2, flat, loose,
+    bank, strain, firsts, turns, mid, mid2, peak, norm, sent, back,
     load_sem, send_sem, recv_sem,
 ):
     g = lax.axis_index("group")
@@ -220,9 +220,9 @@
 
     def place(source, home):
         for i in range(ACROSS):
-            flat[24 * i:24 * i + 4, :] = source(i).astype(F32)
+            loose[4 * i:4 * i + 4, :] = source(i).astype(F32)
         for q in range(4):
-            row = flat[pl.ds(q, ACROSS, stride=24), :]
+            row = loose[pl.ds(q, ACROSS, stride=4), :]
             turned = swapped(row)
             strain[4 * home + q, 0] = jnp.where(left, row, turned)
             strain[4 * home + q, 1] = jnp.where(left, turned, row)
@@ -288,8 +288,11 @@
     best = (peak[...] * jump[0, 40:41, :]).T
     power = norm[...].T
     power = [jnp.sum(power[SIDE * q:SIDE * (q + 1)], axis=0, keepdims=True) for q in range(2)]
-    for k in range(4):
-        sent[k:k + 1, :] = jnp.max(best[32 * k:32 * (k + 1)], axis=0, keepdims=True) / power[k % 2]
+    result = [jnp.max(best[32 * k:32 * (k + 1)], axis=0, keepdims=True) / power[k % 2] for k in range(4)]
+    used = lax.broadcasted_iota(jnp.int32, (1, 128), 1) < 80
+    sent[0:1, :] = jnp.where(used, result[0], pltpu.roll(result[3], 80, 1))
+    sent[1:2, :] = jnp.where(used, result[1], pltpu.roll(result[3], 32, 1))
+    sent[2:3, :] = result[2]
     back[f] = sent[...]
 
     for _, o in far_first((GROUP,)):
@@ -308,10 +311,10 @@
 
     all_shared.wait_recv()
 
-    for i in range(count):
-        for k in range(4):
-            wide[32 * k + i:32 * k + i + 1, :] = back[i, k:k + 1, :]
-    turned = wide[...].T
+    parted = [back[:, k, :] for k in range(3)]
+    lead = lax.broadcasted_iota(jnp.int32, (ACROSS, 128), 1) < 48
+    parted.append(jnp.where(lead, pltpu.roll(parted[0], 48, 1), pltpu.roll(parted[1], 96, 1)))
+    turned = jnp.concatenate(parted, 0).T
     lane = lax.broadcasted_iota(jnp.int32, (8, 128), 1)
     row = lax.broadcasted_iota(jnp.int32, (8, 128), 0)
     for c in range(5):
@@ -360,6 +363,7 @@
             pltpu.VMEM((32, 4, 128), BF16),
             pltpu.VMEM((32, 4, 128), BF16),
             pltpu.VMEM((32 * 24, 128), F32),
+            pltpu.VMEM((32 * 4, 128), F32),
             pltpu.VMEM((PAIRS, 2, ACROSS, 128), F32),
             pltpu.VMEM((SEGS, 2, ACROSS, 128), F32),
             pltpu.VMEM((SEGS, 128, 64), BF16),
@@ -368,9 +372,8 @@
             pltpu.VMEM((4, SIDE, 512), BF16),
             pltpu.VMEM((128, 128), F32),
             pltpu.VMEM((128, 128), F32),
-            pltpu.VMEM((4, 128), F32),
-            pltpu.VMEM((32, 4, 128), F32),
-            pltpu.VMEM((128, 128), F32),
+            pltpu.VMEM((3, 128), F32),
+            pltpu.VMEM((32, 3, 128), F32),
             dma((7,)),
             dma((6,)),
             dma((6,)),

time: 23.8 us -> 23.9 us (level)
  no operation moved by 1% of the time
where the time goes in v8:
time: 23.9 us; the launch traced here: 23.7 us
  Pallas kernels  23.1 us (97%)
  local copies, waits for them, and re-layouts  0.62 us (3%)
    pallas_call x1, Pallas kernels, on_device(): pl.pallas_call(kernel, out_shape=pltpu.VMEM((SEGS, 640), F32), in_specs=[...  23.1 us
    unnamed x1, local copies, waits for them, and re-layouts  0.62 us

profile of v8, /device:TPU:16, one launch (start us, length us, event | category | flops | bytes accessed | tf_op | source)
XLA Modules:
  0.0 23.7 jit_solution(6408547607686407476)
XLA Ops:
  0.0 23.1 %matched_filter.1 = f32[16,640]{1,0:T(8,128)S(1)} custom-call(s32[16]{0:T(128)} %start_hbm.1, bf16[64,2,640]{2,1,0:T(2,128)(2,1)} %tpl_hbm.1, bf16[2,4,64]{2,1,0:T(4,128)(2,1)} %bitcast.3, f32[2,128,64]{2,1,0:T(8,128)} %constant.8.clone.first_hbm, f32[2,128,128]{2,1,0:T(8,128)} %constant.9.clone.turn_hbm, f32[2,48,128]{2,1,0:T(8,128)} %constant.10.clone.jump_hbm, ...), custom_call_target="tpu_custom_call" | custom-call | tf_op jit(solution)/shard_map/matched_filter/pallas_call | solution.py:345
  23.1 0.6 %copy.9 = f32[640,16]{0,1:T(8,128)} copy(f32[640,16]{0,1:T(8,128)S(1)} %bitcast.2) | data formatting | bytes 81920

commit v9 on v7

--- a/solution.py
+++ b/solution.py
@@ -75,8 +75,8 @@
 
 def kernel(
     start_hbm, tpl_hbm, spec_hbm, first_hbm, turn_hbm, jump_hbm, second_hbm, out_ref,
-    start, tpl, spec, first, turn, jump, second, rows, mine, got, other, chunk, beside, beside2, flat,
-    bank, strain, firsts, turns, mid, mid2, peak, norm, sent, back, wide,
+    start, tpl, spec, first, turn, jump, second, rows, mine, got, chunk, wings, flat, loose,
+    bank, strain, firsts, turns, mid, mid2, peak, norm, total, sent, back, wide,
     load_sem, send_sem, recv_sem,
 ):
     g = lax.axis_index("group")
@@ -108,6 +108,9 @@
     barrier = pltpu.get_barrier_semaphore()
     across_g = lax.rem(near + 2, 4)
     late = g // 2
+    core = lax.rem(g, 2)
+    swap = core * (1 - late)
+    other, beside, beside2 = (wings.at[k] for k in range(3))
     group_of = (g, far)
     pl.semaphore_signal(barrier, inc=1, device_id=(far, f), device_id_type=MESH)
     for _, o in far_first((GROUP,)):
@@ -195,7 +198,7 @@
         to_far.wait_recv()
         for _, o in far_first((GROUP,)):
             copy(chunk, beside.at[f], 3, (g, at(o))).start()
-        beside[f] = chunk[...]
+        wings[1, f] = chunk[...]
 
     all_group.wait_recv()
     own_over.start()
@@ -205,24 +208,26 @@
     def swapped(x):
         return pltpu.roll(x, SIDE, 1)
 
-    for i in range(ACROSS):
-        for q in range(5):
-            flat[24 * i + 4 * q:24 * i + 4 * q + 4, :] = got[i, q].astype(F32)
-    for p in range(PAIRS):
-        one = flat[pl.ds(p, ACROSS, stride=24), :]
-        two = flat[pl.ds(p + PAIRS, ACROSS, stride=24), :]
-        re = jnp.where(left, one, swapped(two))
-        im = jnp.where(left, swapped(one), two)
-        bank[p, 0] = re
-        bank[p, 1] = im
-        total = jnp.sum(re * re + im * im, axis=0, keepdims=True)
-        norm[8 * p:8 * (p + 1), :] = jnp.broadcast_to(total, (8, 128))
+    def prepare(u, unpacked):
+        for p in (2 * u, 2 * u + 1):
+            for q in sorted({p // 4, (p + PAIRS) // 4} - unpacked):
+                unpacked.add(q)
+                for i in range(ACROSS):
+                    flat[24 * i + 4 * q:24 * i + 4 * q + 4, :] = got[i, q].astype(F32)
+            one = flat[pl.ds(p, ACROSS, stride=24), :]
+            two = flat[pl.ds(p + PAIRS, ACROSS, stride=24), :]
+            re = jnp.where(left, one, swapped(two))
+            im = jnp.where(left, swapped(one), two)
+            bank[p, 0] = re
+            bank[p, 1] = im
+            level = jnp.sum(re * re + im * im, axis=0, keepdims=True)
+            norm[8 * p:8 * (p + 1), :] = jnp.broadcast_to(level, (8, 128))
 
     def place(source, home):
         for i in range(ACROSS):
-            flat[24 * i:24 * i + 4, :] = source(i).astype(F32)
+            loose[4 * i:4 * i + 4, :] = source(i).astype(F32)
         for q in range(4):
-            row = flat[pl.ds(q, ACROSS, stride=24), :]
+            row = loose[pl.ds(q, ACROSS, stride=4), :]
             turned = swapped(row)
             strain[4 * home + q, 0] = jnp.where(left, row, turned)
             strain[4 * home + q, 1] = jnp.where(left, turned, row)
@@ -252,44 +257,90 @@
             row = 16 * u + 8 * (n // 2) + 2 * home + n % 2
             peak[pl.ds(row, 1), :] = jnp.max(re * re + im * im, axis=0, keepdims=True)
 
-    homes = (g, near, far, across_g)
-    parts = (lambda i: got[i, 5], lambda i: other[i], lambda i: beside[i], lambda i: beside2[i])
-
-    def arrive(n):
-        if n == 1:
-            own_over.wait_recv()
-        if n == 2:
-            @pl.when(late == 0)
-            def _():
-                all_beside.wait_recv()
-
-            @pl.when(late == 1)
-            def _():
-                most_beside.wait_recv()
-
-            far_over.start()
-        if n == 3:
-            far_over.wait_recv()
-
-    steps = [(u, home) for home in range(4) for u in range(PAIRS // 2)]
-    mids = (mid, mid2)
-    for n, (u, home) in enumerate(steps):
-        if u == 0:
-
-            arrive(home)
-
-            place(parts[home], homes[home])
-
-        across(u, homes[home], mids[n % 2])
-        if n > 0:
-            along(steps[n - 1][0], homes[steps[n - 1][1]], mids[(n - 1) % 2])
-    along(steps[-1][0], homes[-1], mids[(len(steps) - 1) % 2])
+    def far_arrived():
+        @pl.when(late == 0)
+        def _():
+            all_beside.wait_recv()
+
+        @pl.when(late == 1)
+        def _():
+            most_beside.wait_recv()
+
+        far_over.start()
+
+    def run(order, arrive):
+        unpacked = set()
+        steps = [(u, n) for n in range(4) for u in range(PAIRS // 2)]
+        mids = (mid, mid2)
+        for step, (u, n) in enumerate(steps):
+            home, part = order[n]
+            if u == 0:
+                arrive(n)
+                place(part, home)
+            if n == 0:
+                prepare(u, unpacked)
+            across(u, home, mids[step % 2])
+            if step > 0:
+                along(steps[step - 1][0], order[steps[step - 1][1]][0], mids[(step - 1) % 2])
+            if step == 12:
+                power = norm[...].T
+                for k in range(2):
+                    total[k:k + 1, :] = jnp.sum(power[SIDE * k:SIDE * (k + 1)], axis=0, keepdims=True)
+        along(PAIRS // 2 - 1, order[3][0], mids[(len(steps) - 1) % 2])
+
+    @pl.when(core == 0)
+    def _():
+        def arrive(n):
+            if n == 0:
+                own_over.wait_recv()
+            if n == 2:
+                far_arrived()
+            if n == 3:
+                far_over.wait_recv()
+
+        run(
+            (
+                (g, lambda i: got[i, 5]), (near, lambda i: wings[0, i]),
+                (far, lambda i: wings[1, i]), (across_g, lambda i: wings[2, i]),
+            ), arrive,
+        )
+
+    @pl.when(core == 1)
+    def _():
+        def arrive(n):
+            if n == 1:
+                @pl.when(late == 1)
+                def _():
+                    own_over.wait_recv()
+
+                @pl.when(late == 0)
+                def _():
+                    all_beside.wait_recv()
+                    far_over.start()
+
+            if n == 2:
+                @pl.when(late == 1)
+                def _():
+                    most_beside.wait_recv()
+                    far_over.start()
+
+                @pl.when(late == 0)
+                def _():
+                    own_over.wait_recv()
+
+            if n == 3:
+                far_over.wait_recv()
+
+        run(
+            (
+                (g, lambda i: got[i, 5]), (near + swap * (far - near), lambda i: wings[swap, i]),
+                (far + swap * (near - far), lambda i: wings[1 - swap, i]), (across_g, lambda i: wings[2, i]),
+            ), arrive,
+        )
 
     best = (peak[...] * jump[0, 40:41, :]).T
-    power = norm[...].T
-    power = [jnp.sum(power[SIDE * q:SIDE * (q + 1)], axis=0, keepdims=True) for q in range(2)]
     for k in range(4):
-        sent[k:k + 1, :] = jnp.max(best[32 * k:32 * (k + 1)], axis=0, keepdims=True) / power[k % 2]
+        sent[k:k + 1, :] = jnp.max(best[32 * k:32 * (k + 1)], axis=0, keepdims=True) / total[k % 2:k % 2 + 1, :]
     back[f] = sent[...]
 
     for _, o in far_first((GROUP,)):
@@ -355,11 +406,10 @@
             pltpu.VMEM((640, 128), F32),
             pltpu.VMEM((32, 6, 4, 128), BF16),
             pltpu.VMEM((32, 6, 4, 128), BF16),
-            pltpu.VMEM((32, 4, 128), BF16),
             pltpu.VMEM((4, 128), BF16),
-            pltpu.VMEM((32, 4, 128), BF16),
-            pltpu.VMEM((32, 4, 128), BF16),
+            pltpu.VMEM((3, 32, 4, 128), BF16),
             pltpu.VMEM((32 * 24, 128), F32),
+            pltpu.VMEM((32 * 4, 128), F32),
             pltpu.VMEM((PAIRS, 2, ACROSS, 128), F32),
             pltpu.VMEM((SEGS, 2, ACROSS, 128), F32),
             pltpu.VMEM((SEGS, 128, 64), BF16),
@@ -368,6 +418,7 @@
             pltpu.VMEM((4, SIDE, 512), BF16),
             pltpu.VMEM((128, 128), F32),
             pltpu.VMEM((128, 128), F32),
+            pltpu.VMEM((2, 128), F32),
             pltpu.VMEM((4, 128), F32),
             pltpu.VMEM((32, 4, 128), F32),
             pltpu.VMEM((128, 128), F32),

time: 23.8 us -> 23.8 us (level)
  no operation moved by 1% of the time
where the time goes in v9:
time: 23.8 us; the launch traced here: 23.5 us
  Pallas kernels  22.8 us (96%)
  local copies, waits for them, and re-layouts  0.62 us (3%)
    pallas_call x1, Pallas kernels, on_device(): pl.pallas_call(kernel, out_shape=pltpu.VMEM((SEGS, 640), F32), in_specs=[...  22.8 us
    unnamed x1, local copies, waits for them, and re-layouts  0.62 us

profile of v9, /device:TPU:16, one launch (start us, length us, event | category | flops | bytes accessed | tf_op | source)
XLA Modules:
  0.0 23.5 jit_solution(16549312842245626089)
XLA Ops:
  0.0 22.8 %matched_filter.1 = f32[16,640]{1,0:T(8,128)S(1)} custom-call(s32[16]{0:T(128)} %start_hbm.1, bf16[64,2,640]{2,1,0:T(2,128)(2,1)} %tpl_hbm.1, bf16[2,4,64]{2,1,0:T(4,128)(2,1)} %bitcast.3, f32[2,128,64]{2,1,0:T(8,128)} %constant.8.clone.first_hbm, f32[2,128,128]{2,1,0:T(8,128)} %constant.9.clone.turn_hbm, f32[2,48,128]{2,1,0:T(8,128)} %constant.10.clone.jump_hbm, ...), custom_call_target="tpu_custom_call" | custom-call | tf_op jit(solution)/shard_map/matched_filter/pallas_call | solution.py:393
  22.9 0.6 %copy.9 = f32[640,16]{0,1:T(8,128)} copy(f32[640,16]{0,1:T(8,128)S(1)} %bitcast.2) | data formatting | bytes 81920

commit v10 on v9

--- a/solution.py
+++ b/solution.py
@@ -67,7 +67,11 @@
 
     offsets = [(dz, dx, dy) for dz in range(4) for dx in range(4) for dy in range(2)]
     entries = [(kind, o) for o in offsets for kind in kinds if (kind, o) != (GROUP, (0, 0, 0))]
-    return sorted(entries, key=lambda entry: (-hops(entry), kinds.index(entry[0])))
+    def order(entry):
+        (kind, (dz, dx, _)) = entry
+        return -hops(entry) - 0.6 * (dz == 3) - 0.6 * (dx == 3), kinds.index(kind)
+
+    return sorted(entries, key=order)
 
 
 GROUP, FAR = range(2)

time: 23.8 us -> 23.5 us (0.987)
  no operation moved by 1% of the time
where the time goes in v10:
time: 23.5 us; the launch traced here: 23.4 us
  Pallas kernels  22.7 us (97%)
  local copies, waits for them, and re-layouts  0.62 us (3%)
    pallas_call x1, Pallas kernels, on_device(): pl.pallas_call(kernel, out_shape=pltpu.VMEM((SEGS, 640), F32), in_specs=[...  22.7 us
    unnamed x1, local copies, waits for them, and re-layouts  0.62 us

profile of v10, /device:TPU:16, one launch (start us, length us, event | category | flops | bytes accessed | tf_op | source)
XLA Modules:
  0.0 23.4 jit_solution(10242308791673270825)
XLA Ops:
  0.0 22.7 %matched_filter.1 = f32[16,640]{1,0:T(8,128)S(1)} custom-call(s32[16]{0:T(128)} %start_hbm.1, bf16[64,2,640]{2,1,0:T(2,128)(2,1)} %tpl_hbm.1, bf16[2,4,64]{2,1,0:T(4,128)(2,1)} %bitcast.3, f32[2,128,64]{2,1,0:T(8,128)} %constant.8.clone.first_hbm, f32[2,128,128]{2,1,0:T(8,128)} %constant.9.clone.turn_hbm, f32[2,48,128]{2,1,0:T(8,128)} %constant.10.clone.jump_hbm, ...), custom_call_target="tpu_custom_call" | custom-call | tf_op jit(solution)/shard_map/matched_filter/pallas_call | solution.py:397
  22.7 0.6 %copy.9 = f32[640,16]{0,1:T(8,128)} copy(f32[640,16]{0,1:T(8,128)S(1)} %bitcast.2) | data formatting | bytes 81920

commit v11 on v10

--- a/solution.py
+++ b/solution.py
@@ -60,7 +60,7 @@
     return jnp.asarray(first, F32), jnp.asarray(turn, F32), jnp.asarray(jump, F32), jnp.asarray(second, BF16)
 
 
-def far_first(kinds):
+def far_first(kinds, first=3):
     def hops(entry):
         (kind, (dz, dx, dy)) = entry
         return min(dz, 4 - dz) + min(dx, 4 - dx) + (2 - dy if kind == FAR else dy)
@@ -69,7 +69,7 @@
     entries = [(kind, o) for o in offsets for kind in kinds if (kind, o) != (GROUP, (0, 0, 0))]
     def order(entry):
         (kind, (dz, dx, _)) = entry
-        return -hops(entry) - 0.6 * (dz == 3) - 0.6 * (dx == 3), kinds.index(kind)
+        return -hops(entry) - 0.6 * (dz == first) - 0.6 * (dx == first), kinds.index(kind)
 
     return sorted(entries, key=order)
 
@@ -117,13 +117,13 @@
     other, beside, beside2 = (wings.at[k] for k in range(3))
     group_of = (g, far)
     pl.semaphore_signal(barrier, inc=1, device_id=(far, f), device_id_type=MESH)
-    for _, o in far_first((GROUP,)):
+    for _, o in far_first((GROUP,), 1):
         pl.semaphore_signal(barrier, inc=1, device_id=(g, at(o)), device_id_type=MESH)
     pl.semaphore_signal(barrier, inc=1, device_id=(near, f), device_id_type=MESH)
 
     @pl.when(late == 0)
     def _():
-        for _, o in far_first((FAR,)):
+        for _, o in far_first((FAR,), 1):
             if o != (0, 0, 0):
                 pl.semaphore_signal(barrier, inc=1, device_id=(far, at(o)), device_id_type=MESH)
 
@@ -347,7 +347,7 @@
         sent[k:k + 1, :] = jnp.max(best[32 * k:32 * (k + 1)], axis=0, keepdims=True) / total[k % 2:k % 2 + 1, :]
     back[f] = sent[...]
 
-    for _, o in far_first((GROUP,)):
+    for _, o in far_first((GROUP,), 1):
         copy(sent, back.at[f], 5, (g, at(o))).start()
     for whole in (all_group, own_over, far_over):
         whole.wait_send()

time: 23.5 us -> 23.4 us (level)
  no operation moved by 1% of the time
where the time goes in v11:
time: 23.4 us; the launch traced here: 23.2 us
  Pallas kernels  22.6 us (97%)
  local copies, waits for them, and re-layouts  0.62 us (3%)
    pallas_call x1, Pallas kernels, on_device(): pl.pallas_call(kernel, out_shape=pltpu.VMEM((SEGS, 640), F32), in_specs=[...  22.6 us
    unnamed x1, local copies, waits for them, and re-layouts  0.62 us

profile of v11, /device:TPU:16, one launch (start us, length us, event | category | flops | bytes accessed | tf_op | source)
XLA Modules:
  0.0 23.2 jit_solution(9438018866367077882)
XLA Ops:
  0.0 22.6 %matched_filter.1 = f32[16,640]{1,0:T(8,128)S(1)} custom-call(s32[16]{0:T(128)} %start_hbm.1, bf16[64,2,640]{2,1,0:T(2,128)(2,1)} %tpl_hbm.1, bf16[2,4,64]{2,1,0:T(4,128)(2,1)} %bitcast.3, f32[2,128,64]{2,1,0:T(8,128)} %constant.8.clone.first_hbm, f32[2,128,128]{2,1,0:T(8,128)} %constant.9.clone.turn_hbm, f32[2,48,128]{2,1,0:T(8,128)} %constant.10.clone.jump_hbm, ...), custom_call_target="tpu_custom_call" | custom-call | tf_op jit(solution)/shard_map/matched_filter/pallas_call | solution.py:397
  22.6 0.6 %copy.9 = f32[640,16]{0,1:T(8,128)} copy(f32[640,16]{0,1:T(8,128)S(1)} %bitcast.2) | data formatting | bytes 81920

commit v12 on v11

--- a/solution.py
+++ b/solution.py
@@ -69,7 +69,7 @@
     entries = [(kind, o) for o in offsets for kind in kinds if (kind, o) != (GROUP, (0, 0, 0))]
     def order(entry):
         (kind, (dz, dx, _)) = entry
-        return -hops(entry) - 0.6 * (dz == first) - 0.6 * (dx == first), kinds.index(kind)
+        return -hops(entry) - 0.45 * (dz == first) - 0.45 * (dx == first), kinds.index(kind)
 
     return sorted(entries, key=order)
 

time: 23.4 us -> 23.4 us (level)
  no operation moved by 1% of the time
where the time goes in v12:
time: 23.4 us; the launch traced here: 23.3 us
  Pallas kernels  22.7 us (97%)
  local copies, waits for them, and re-layouts  0.62 us (3%)
    pallas_call x1, Pallas kernels, on_device(): pl.pallas_call(kernel, out_shape=pltpu.VMEM((SEGS, 640), F32), in_specs=[...  22.7 us
    unnamed x1, local copies, waits for them, and re-layouts  0.62 us

profile of v12, /device:TPU:16, one launch (start us, length us, event | category | flops | bytes accessed | tf_op | source)
XLA Modules:
  0.0 23.3 jit_solution(8785095433245286363)
XLA Ops:
  0.0 22.7 %matched_filter.1 = f32[16,640]{1,0:T(8,128)S(1)} custom-call(s32[16]{0:T(128)} %start_hbm.1, bf16[64,2,640]{2,1,0:T(2,128)(2,1)} %tpl_hbm.1, bf16[2,4,64]{2,1,0:T(4,128)(2,1)} %bitcast.3, f32[2,128,64]{2,1,0:T(8,128)} %constant.8.clone.first_hbm, f32[2,128,128]{2,1,0:T(8,128)} %constant.9.clone.turn_hbm, f32[2,48,128]{2,1,0:T(8,128)} %constant.10.clone.jump_hbm, ...), custom_call_target="tpu_custom_call" | custom-call | tf_op jit(solution)/shard_map/matched_filter/pallas_call | solution.py:397
  22.7 0.6 %copy.9 = f32[640,16]{0,1:T(8,128)} copy(f32[640,16]{0,1:T(8,128)S(1)} %bitcast.2) | data formatting | bytes 81920

commit v13 on v11

--- a/solution.py
+++ b/solution.py
@@ -80,7 +80,7 @@
 def kernel(
     start_hbm, tpl_hbm, spec_hbm, first_hbm, turn_hbm, jump_hbm, second_hbm, out_ref,
     start, tpl, spec, first, turn, jump, second, rows, mine, got, chunk, wings, flat, loose,
-    bank, strain, firsts, turns, mid, mid2, peak, norm, total, sent, back, wide,
+    bank, strain, firsts, turns, mid, mid2, peak, norm, total, sent, back,
     load_sem, send_sem, recv_sem,
 ):
     g = lax.axis_index("group")
@@ -363,10 +363,7 @@
 
     all_shared.wait_recv()
 
-    for i in range(count):
-        for k in range(4):
-            wide[32 * k + i:32 * k + i + 1, :] = back[i, k:k + 1, :]
-    turned = wide[...].T
+    turned = jnp.concatenate([back[:, k, :] for k in range(4)], 0).T
     lane = lax.broadcasted_iota(jnp.int32, (8, 128), 1)
     row = lax.broadcasted_iota(jnp.int32, (8, 128), 0)
     for c in range(5):
@@ -425,7 +422,6 @@
             pltpu.VMEM((2, 128), F32),
             pltpu.VMEM((4, 128), F32),
             pltpu.VMEM((32, 4, 128), F32),
-            pltpu.VMEM((128, 128), F32),
             dma((7,)),
             dma((6,)),
             dma((6,)),

time: 23.4 us -> 23.3 us (level)
  no operation moved by 1% of the time
where the time goes in v13:
time: 23.3 us; the launch traced here: 23.2 us
  Pallas kernels  22.6 us (97%)
  local copies, waits for them, and re-layouts  0.62 us (3%)
    pallas_call x1, Pallas kernels, on_device(): pl.pallas_call(kernel, out_shape=pltpu.VMEM((SEGS, 640), F32), in_specs=[...  22.6 us
    unnamed x1, local copies, waits for them, and re-layouts  0.62 us

profile of v13, /device:TPU:16, one launch (start us, length us, event | category | flops | bytes accessed | tf_op | source)
XLA Modules:
  0.0 23.2 jit_solution(235882479369970276)
XLA Ops:
  0.0 22.6 %matched_filter.1 = f32[16,640]{1,0:T(8,128)S(1)} custom-call(s32[16]{0:T(128)} %start_hbm.1, bf16[64,2,640]{2,1,0:T(2,128)(2,1)} %tpl_hbm.1, bf16[2,4,64]{2,1,0:T(4,128)(2,1)} %bitcast.3, f32[2,128,64]{2,1,0:T(8,128)} %constant.8.clone.first_hbm, f32[2,128,128]{2,1,0:T(8,128)} %constant.9.clone.turn_hbm, f32[2,48,128]{2,1,0:T(8,128)} %constant.10.clone.jump_hbm, ...), custom_call_target="tpu_custom_call" | custom-call | tf_op jit(solution)/shard_map/matched_filter/pallas_call | solution.py:394
  22.6 0.6 %copy.9 = f32[640,16]{0,1:T(8,128)} copy(f32[640,16]{0,1:T(8,128)S(1)} %bitcast.2) | data formatting | bytes 81920
